TPU v7x, 128 devices: a whole 4x4x4 slice. The times are simulated.
128 devices in a mesh: fsdp: 8 (over x, y_lo), tensor: 16 (over z, y_hi, core).
Axes of the slice: x: 4, y: 4 (y_hi: 2, y_lo: 2; y = y_hi * 2 + y_lo), z: 4, core: 2. Of those that a mesh axis runs over, the one named last changes fastest.
Arguments:
- modality: int32 [8192], P('fsdp'), may hold values from 0 to 2, as said below
- out_grad: bfloat16 [8192, 4096], P('fsdp', 'tensor'), may hold values from -6 to 6
- gate_pre: bfloat16 [8192, 11008], P('fsdp', 'tensor'), may hold values from -6 to 6
- up_pre: bfloat16 [8192, 11008], P('fsdp', 'tensor'), may hold values from -6 to 6
- down_weight: bfloat16 [3, 11008, 4096], P(None, 'tensor', 'fsdp'), may hold values from -0.0546875 to 0.0546875
Outputs:
- down_grad: float32 [3, 11008, 4096], P(None, 'tensor', 'fsdp')
- gate_grad: bfloat16 [8192, 11008], P('fsdp', 'tensor')
- up_grad: bfloat16 [8192, 11008], P('fsdp', 'tensor')
Inputs may be any that keep to these rules, and one draw needn't show every extreme that they name: `modality`: the 1024 tokens of every index of fsdp hold each of the three modalities at least once.
All inputs are finite; a program needn't handle non-finite values.
Results may differ from a plain program's by a relative error of at most 0.012.
Values may be sent and summed in bfloat16 or wider, within the bound.
A program may use at most 256 MiB of HBM per device.

v0:
```python
import math

import jax
import jax.numpy as jnp
from jax import lax
from jax.sharding import Mesh
from jax.sharding import PartitionSpec as P

FSDP = ("fsdp_0", "fsdp_1")


def sent_to_all(shard, axis):
    peers = lax.axis_size(axis)
    return lax.all_to_all(
        jnp.broadcast_to(shard[None], (peers, *shard.shape)), axis, 0, 0, tiled=True
    )


def taken_together(shard, axis):
    return sent_to_all(shard, axis).sum(axis=0)


def gather_axes(shard, axes, dim):
    for axis in reversed(axes):
        shard = lax.all_gather(shard, axis, axis=dim, tiled=True)
    return shard


def sum_by_axis(shard, axes, dim):
    for axis in axes:
        shard = lax.psum_scatter(shard, axis, scatter_dimension=dim, tiled=True)
    return shard


def kind_table(kind_ids):
    labels = jnp.arange(3, dtype=jnp.int32)
    return (kind_ids[:, None] == labels[None, :]).astype(jnp.float32)


def shards(modality, out_grad, gate_pre, up_pre, down_weight):
    tok_rows = modality.shape[0]
    groups = lax.axis_size(FSDP)
    local_onehot = kind_table(modality)
    counts = taken_together(jnp.sum(local_onehot, axis=0), FSDP)
    factor = tok_rows * groups / (3.0 * counts)
    token_scale = jnp.sum(local_onehot * factor[None, :], axis=1)
    scaled_part = (out_grad.astype(jnp.float32) * token_scale[:, None]).astype(jnp.bfloat16)
    scaled = lax.all_gather(scaled_part, "tensor", axis=1, tiled=True)
    gate_val = gate_pre.astype(jnp.float32)
    up_val = up_pre.astype(jnp.float32)
    sigmoid_g = jax.nn.sigmoid(gate_val)
    active = gate_val * sigmoid_g
    hidden = (active * up_val).astype(jnp.bfloat16)
    hid_cols = hidden.shape[1]
    width_all = scaled.shape[1]
    block_rows = math.gcd(tok_rows, 128)
    block_count = tok_rows // block_rows + 2
    capacity = block_count * block_rows
    int_onehot = local_onehot.astype(jnp.int32)
    slot_rank = jnp.sum((jnp.cumsum(int_onehot, axis=0) - int_onehot) * int_onehot, axis=1)
    used_rows = jnp.sum(int_onehot, axis=0)
    padded = (used_rows + block_rows - 1) // block_rows * block_rows
    second = padded[0]
    third_start = padded[0] + padded[1]
    starts = jnp.stack([jnp.zeros((), jnp.int32), second, third_start])
    slot_index = jnp.sum(int_onehot * starts[None, :], axis=1) + slot_rank
    block_first = jnp.arange(block_count, dtype=jnp.int32) * block_rows
    block_kind = (block_first >= second).astype(jnp.int32) + (block_first >= third_start).astype(
        jnp.int32
    )
    packed_scaled = jnp.zeros((capacity, width_all), jnp.bfloat16).at[slot_index].set(scaled)
    packed_hidden = jnp.zeros((capacity, hid_cols), jnp.bfloat16).at[slot_index].set(hidden)
    weight_piece = gather_axes(down_weight, FSDP, 2)
    columns_here = weight_piece.shape[2]
    columns = packed_scaled
    columns = columns.reshape(block_count, block_rows, columns_here)
    chosen = jnp.take(weight_piece, block_kind, axis=0)
    product = jnp.einsum("bkw,bfw->bkf", columns, chosen, preferred_element_type=jnp.float32)
    folded = product.reshape(capacity, hid_cols)
    d_hidden = folded[slot_index]
    up_grad = (d_hidden * active).astype(jnp.bfloat16)
    slope = sigmoid_g * (1.0 + gate_val * (1.0 - sigmoid_g))
    gate_grad = (d_hidden * up_val * slope).astype(jnp.bfloat16)

    def kind_product(kind_id):
        first_block = starts[kind_id] // block_rows
        last_block = first_block + padded[kind_id] // block_rows

        def add_block(block_index, running):
            rows_hidden = lax.dynamic_slice_in_dim(
                packed_hidden, block_index * block_rows, block_rows, 0
            )
            rows_scaled = lax.dynamic_slice_in_dim(
                packed_scaled, block_index * block_rows, block_rows, 0
            )
            return running + lax.dot_general(
                rows_hidden,
                rows_scaled,
                (((0,), (0,)), ((), ())),
                preferred_element_type=jnp.float32,
            )

        return lax.fori_loop(
            first_block, last_block, add_block, jnp.zeros((hid_cols, width_all), jnp.float32)
        )

    partial_sum = jnp.stack([kind_product(kind_id) for kind_id in range(3)])
    down_grad = sum_by_axis(partial_sum.astype(jnp.bfloat16), FSDP, 2).astype(jnp.float32)
    return (down_grad, gate_grad, up_grad)


def solution(mesh):
    torus = Mesh(mesh.devices.reshape(4, 2, mesh.shape["tensor"]), ("fsdp_0", "fsdp_1", "tensor"))
    in_specs = (
        P(FSDP),
        P(FSDP, "tensor"),
        P(FSDP, "tensor"),
        P(FSDP, "tensor"),
        P(None, "tensor", FSDP),
    )
    out_specs = (P(None, "tensor", FSDP), P(FSDP, "tensor"), P(FSDP, "tensor"))
    return jax.shard_map(
        shards, mesh=torus, in_specs=in_specs, out_specs=out_specs, check_vma=False
    )
```

profile of v0, /device:TPU:0, one launch (start us, length us, event | category | flops | bytes accessed | tf_op | source)
XLA Modules:
  0.0 535.3 jit_solution(230502349124138979)
XLA Ops:
  7.2 0.7 all-gather.6.cloned.1.call-update
  7.9 0.8 convert_reduce_fusion
  9.3 5.4 %all-to-all-start = ((f32[8,1,3]{2,1,0:T(1,128)}), f32[8,1,3]{2,1,0:T(1,128)S(1)}, u32[]{:S(2)}, u32[]{:S(2)}) async-start(f32[8,1,3]{2,1,0:T(1,128)} %broadcast_in_dim.15), calls=%async_computation | async-start | bytes 8192 | tf_op jit(solution)/shard_map/all_to_all | solution.py:14
  14.8 6.1 %all-to-all-done = f32[8,1,3]{2,1,0:T(1,128)S(1)} async-done(((f32[8,1,3]{2,1,0:T(1,128)}), f32[8,1,3]{2,1,0:T(1,128)S(1)}, u32[]{:S(2)}, u32[]{:S(2)}) %all-to-all-start) | async-done | bytes 128 | tf_op jit(solution)/shard_map/all_to_all | solution.py:14
  20.9 0.8 select_reduce_fusion
  21.7 2.1 multiply_convert_fusion.1
  23.9 47.9 %all-gather.6.cloned.1.call-done = bf16[3,688,1024]{2,1,0:T(8,128)(2,1)} async-done(((bf16[3,688,512]{2,1,0:T(8,128)(2,1)}), bf16[3,688,1024]{2,1,0:T(8,128)(2,1)}) %all-gather.6.cloned.1.call-update) | async-done | bytes 4227088 | tf_op jit(solution)/shard_map/all_gather | solution.py:25
  72.0 0.7 fusion.40
  81.6 0.9 reduce-window.6
  82.9 0.7 copy.28
  83.6 2.2 copy.29
  85.9 0.7 pad_add_fusion
  86.8 7.4 %scatter_custom_fusion = bf16[1280,688]{1,0:T(8,128)(2,1)} fusion(s32[1024]{0:T(1024)S(1)} %bitcast.34, bf16[1024,688]{1,0:T(8,128)(2,1)S(1)} %copy.29, bf16[1024,688]{1,0:T(8,128)(2,1)S(1)} %copy.28, f32[]{:T(128)} %constant.119.clone.1, bf16[]{:T(256)} %constant.116.clone.1), kind=kCustom, calls=%fused_computation.46 | custom fusion | flops 5636096 | bytes 4907014 | tf_op jit(solution)/shard_map/scatter | solution.py:72
  94.2 58.0 %all-gather.4.cloned.1.call-done = bf16[1024,4096]{1,0:T(8,128)(2,1)} async-done(((bf16[1024,256]{1,0:T(8,128)(2,1)}), bf16[1024,4096]{1,0:T(8,128)(2,1)}) %all-gather.4.cloned.1.call-update) | async-done | bytes 8388624 | tf_op jit(solution)/shard_map/all_gather | solution.py:48
  152.3 19.3 %scatter_custom_fusion.1 = bf16[1280,4096]{1,0:T(8,128)(2,1)} fusion(s32[1024]{0:T(1024)S(1)} %bitcast.35, bf16[1024,4096]{1,0:T(8,128)(2,1)} %all-gather.4.cloned.1.call-done, bf16[]{:T(256)} %constant.116.clone.1), kind=kCustom, calls=%fused_computation.30 | custom fusion | bytes 10486272 | tf_op jit(solution)/shard_map/scatter | solution.py:71
  171.6 5.6 %broadcast.148.clone.2 = f32[688,4096]{1,0:T(8,128)} broadcast(f32[]{:T(128)} %constant.110.clone.1), dimensions={} | broadcast | bytes 11272196 | tf_op jit(solution)/shard_map/broadcast.21
  177.3 21.1 %while.30 = (s32[]{:T(128)}, f32[688,4096]{1,0:T(8,128)}, s32[]{:T(128)}, bf16[1280,688]{1,0:T(8,128)(2,1)}, bf16[1280,4096]{1,0:T(8,128)(2,1)}, /*index=5*/s32[]{:T(128)}, s32[]{:T(128)}, s32[]{:T(128)}, s32[]{:T(128)}) while((s32[]{:T(128)}, f32[688,4096]{1,0:T(8,128)}, s32[]{:T(128)}, bf16[1280,688]{1,0:T(8,128)(2,1)}, ...), condition=%wide.region_11.12_spmd, body=%wide.region_10.11_spmd.sunk | while | flops 724238336 | bytes 23790732 | solution.py:103
  177.3 10.5 %convolution_add_fusion.6 = f32[688,4096]{1,0:T(8,128)} fusion(f32[688,4096]{1,0:T(8,128)} %get-tuple-element.306, bf16[1280,4096]{1,0:T(8,128)(2,1)} %get-tuple-element.318, s32[]{:T(128)S(6)} %select_n.91, bf16[1280,688]{1,0:T(8,128)(2,1)} %get-tuple-element.317), kind=kOutput, calls=%fused_computation.6.clone.1 | convolution fusion | flops 724238336 | bytes 23790592 | tf_op jit(solution)/shard_map/while/body/dot_general | solution.py:96
  187.8 10.6 %convolution_add_fusion.6 = f32[688,4096]{1,0:T(8,128)} fusion(f32[688,4096]{1,0:T(8,128)} %get-tuple-element.306, bf16[1280,4096]{1,0:T(8,128)(2,1)} %get-tuple-element.318, s32[]{:T(128)S(6)} %select_n.91, bf16[1280,688]{1,0:T(8,128)(2,1)} %get-tuple-element.317), kind=kOutput, calls=%fused_computation.6.clone.1 | convolution fusion | flops 724238336 | bytes 23790592 | tf_op jit(solution)/shard_map/while/body/dot_general | solution.py:96
  198.3 7.7 %convert_bitcast_fusion.2 = bf16[1,688,4096]{2,1,0:T(8,128)(2,1)} fusion(f32[688,4096]{1,0:T(8,128)} %get-tuple-element.87), kind=kLoop, calls=%fused_computation.29 | loop fusion | flops 2818048 | bytes 16908288 | tf_op jit(solution)/shard_map/stack | solution.py:107
  206.0 5.5 %broadcast.148.clone.1 = f32[688,4096]{1,0:T(8,128)} broadcast(f32[]{:T(128)} %constant.110.clone.1), dimensions={} | broadcast | bytes 11272196 | tf_op jit(solution)/shard_map/broadcast.21
  211.5 63.1 %while.31 = (s32[]{:T(128)}, f32[688,4096]{1,0:T(8,128)}, s32[]{:T(128)}, bf16[1280,688]{1,0:T(8,128)(2,1)}, bf16[1280,4096]{1,0:T(8,128)(2,1)}, /*index=5*/s32[]{:T(128)}, s32[]{:T(128)}, s32[]{:T(128)}, s32[]{:T(128)}) while((s32[]{:T(128)}, f32[688,4096]{1,0:T(8,128)}, s32[]{:T(128)}, bf16[1280,688]{1,0:T(8,128)(2,1)}, ...), condition=%wide.region_13.14_spmd, body=%wide.region_12.13_spmd.sunk | while | flops 724238336 | bytes 23790732 | solution.py:103
  211.5 10.4 %convolution_add_fusion.7 = f32[688,4096]{1,0:T(8,128)} fusion(f32[688,4096]{1,0:T(8,128)} %get-tuple-element.279, bf16[1280,4096]{1,0:T(8,128)(2,1)} %get-tuple-element.291, s32[]{:T(128)S(6)} %select_n.92, bf16[1280,688]{1,0:T(8,128)(2,1)} %get-tuple-element.290), kind=kOutput, calls=%fused_computation.10.clone.1 | convolution fusion | flops 724238336 | bytes 23790592 | tf_op jit(solution)/shard_map/while/body/dot_general | solution.py:96
  221.9 10.4 %convolution_add_fusion.7 = f32[688,4096]{1,0:T(8,128)} fusion(f32[688,4096]{1,0:T(8,128)} %get-tuple-element.279, bf16[1280,4096]{1,0:T(8,128)(2,1)} %get-tuple-element.291, s32[]{:T(128)S(6)} %select_n.92, bf16[1280,688]{1,0:T(8,128)(2,1)} %get-tuple-element.290), kind=kOutput, calls=%fused_computation.10.clone.1 | convolution fusion | flops 724238336 | bytes 23790592 | tf_op jit(solution)/shard_map/while/body/dot_general | solution.py:96
  232.4 10.5 %convolution_add_fusion.7 = f32[688,4096]{1,0:T(8,128)} fusion(f32[688,4096]{1,0:T(8,128)} %get-tuple-element.279, bf16[1280,4096]{1,0:T(8,128)(2,1)} %get-tuple-element.291, s32[]{:T(128)S(6)} %select_n.92, bf16[1280,688]{1,0:T(8,128)(2,1)} %get-tuple-element.290), kind=kOutput, calls=%fused_computation.10.clone.1 | convolution fusion | flops 724238336 | bytes 23790592 | tf_op jit(solution)/shard_map/while/body/dot_general | solution.py:96
  242.9 10.5 %convolution_add_fusion.7 = f32[688,4096]{1,0:T(8,128)} fusion(f32[688,4096]{1,0:T(8,128)} %get-tuple-element.279, bf16[1280,4096]{1,0:T(8,128)(2,1)} %get-tuple-element.291, s32[]{:T(128)S(6)} %select_n.92, bf16[1280,688]{1,0:T(8,128)(2,1)} %get-tuple-element.290), kind=kOutput, calls=%fused_computation.10.clone.1 | convolution fusion | flops 724238336 | bytes 23790592 | tf_op jit(solution)/shard_map/while/body/dot_general | solution.py:96
  253.4 10.6 %convolution_add_fusion.7 = f32[688,4096]{1,0:T(8,128)} fusion(f32[688,4096]{1,0:T(8,128)} %get-tuple-element.279, bf16[1280,4096]{1,0:T(8,128)(2,1)} %get-tuple-element.291, s32[]{:T(128)S(6)} %select_n.92, bf16[1280,688]{1,0:T(8,128)(2,1)} %get-tuple-element.290), kind=kOutput, calls=%fused_computation.10.clone.1 | convolution fusion | flops 724238336 | bytes 23790592 | tf_op jit(solution)/shard_map/while/body/dot_general | solution.py:96
  264.0 10.6 %convolution_add_fusion.7 = f32[688,4096]{1,0:T(8,128)} fusion(f32[688,4096]{1,0:T(8,128)} %get-tuple-element.279, bf16[1280,4096]{1,0:T(8,128)(2,1)} %get-tuple-element.291, s32[]{:T(128)S(6)} %select_n.92, bf16[1280,688]{1,0:T(8,128)(2,1)} %get-tuple-element.290), kind=kOutput, calls=%fused_computation.10.clone.1 | convolution fusion | flops 724238336 | bytes 23790592 | tf_op jit(solution)/shard_map/while/body/dot_general | solution.py:96
  274.6 5.6 %broadcast.148.clone = f32[688,4096]{1,0:T(8,128)} broadcast(f32[]{:T(128)} %constant.110.clone.1), dimensions={} | broadcast | bytes 11272196 | tf_op jit(solution)/shard_map/broadcast.21
  280.3 21.0 %while.32 = (s32[]{:T(128)}, f32[688,4096]{1,0:T(8,128)}, s32[]{:T(128)}, bf16[1280,688]{1,0:T(8,128)(2,1)}, bf16[1280,4096]{1,0:T(8,128)(2,1)}, /*index=5*/s32[]{:T(128)}, s32[]{:T(128)}, s32[]{:T(128)}, s32[]{:T(128)}) while((s32[]{:T(128)}, f32[688,4096]{1,0:T(8,128)}, s32[]{:T(128)}, bf16[1280,688]{1,0:T(8,128)(2,1)}, ...), condition=%wide.region_15.16_spmd, body=%wide.region_14.15_spmd.sunk | while | flops 724238336 | bytes 23790732 | solution.py:103
  280.3 10.5 %convolution_add_fusion.8 = f32[688,4096]{1,0:T(8,128)} fusion(f32[688,4096]{1,0:T(8,128)} %get-tuple-element.252, bf16[1280,4096]{1,0:T(8,128)(2,1)} %get-tuple-element.264, s32[]{:T(128)S(6)} %select_n.93, bf16[1280,688]{1,0:T(8,128)(2,1)} %get-tuple-element.263), kind=kOutput, calls=%fused_computation.14.clone.1 | convolution fusion | flops 724238336 | bytes 23790592 | tf_op jit(solution)/shard_map/while/body/dot_general | solution.py:96
  290.7 10.5 %convolution_add_fusion.8 = f32[688,4096]{1,0:T(8,128)} fusion(f32[688,4096]{1,0:T(8,128)} %get-tuple-element.252, bf16[1280,4096]{1,0:T(8,128)(2,1)} %get-tuple-element.264, s32[]{:T(128)S(6)} %select_n.93, bf16[1280,688]{1,0:T(8,128)(2,1)} %get-tuple-element.263), kind=kOutput, calls=%fused_computation.14.clone.1 | convolution fusion | flops 724238336 | bytes 23790592 | tf_op jit(solution)/shard_map/while/body/dot_general | solution.py:96
  301.2 8.3 %convert_bitcast_fusion = (bf16[1,688,4096]{2,1,0:T(8,128)(2,1)S(1)}, bf16[1,688,4096]{2,1,0:T(8,128)(2,1)S(1)}) fusion(f32[688,4096]{1,0:T(8,128)} %get-tuple-element.89, f32[688,4096]{1,0:T(8,128)} %get-tuple-element.88), kind=kLoop, calls=%fused_computation.27 | loop fusion | flops 5636096 | bytes 33816576 | tf_op jit(solution)/shard_map/stack | solution.py:107
  309.5 10.1 %pad_maximum_fusion = bf16[3,688,4096]{2,1,0:T(8,128)(2,1)} fusion(bf16[1,688,4096]{2,1,0:T(8,128)(2,1)S(1)} %get-tuple-element.144, bf16[1,688,4096]{2,1,0:T(8,128)(2,1)S(1)} %get-tuple-element.145, bf16[1,688,4096]{2,1,0:T(8,128)(2,1)} %convert_bitcast_fusion.2), kind=kLoop, calls=%fused_computation.26 | loop fusion | flops 16908288 | bytes 33816576 | tf_op jit(solution)/shard_map/stack | solution.py:107
  320.6 0.6 compare_and_fusion
  321.8 9.9 %fusion.39 = (bf16[3,688,1408]{2,1,0:T(8,128)(2,1)}, bf16[3,688,1408]{2,1,0:T(8,128)(2,1)}) fusion(bf16[3,688,4096]{2,1,0:T(8,128)(2,1)} %all-gather.8.cloned.1.call-done), kind=kLoop, calls=%fused_computation.85 | loop fusion | bytes 23248896 | tf_op jit(solution)/shard_map/jit(_take)/gather | solution.py:77
  331.7 14.3 %gather_fusion.1 = bf16[10,688,1408]{2,1,0:T(8,128)(2,1)} fusion(bf16[3,688,1408]{2,1,0:T(8,128)(2,1)} %get-tuple-element.137, s32[1024]{0:T(1024)S(1)} %pad_clamp_fusion), kind=kCustom, calls=%fused_computation.1 | custom fusion | bytes 38748200 | tf_op jit(solution)/shard_map/jit(_take)/gather | solution.py:77
  346.0 14.5 %gather_fusion.2 = bf16[10,688,1408]{2,1,0:T(8,128)(2,1)} fusion(bf16[3,688,1408]{2,1,0:T(8,128)(2,1)} %get-tuple-element.138, s32[1024]{0:T(1024)S(1)} %pad_clamp_fusion), kind=kCustom, calls=%fused_computation.2 | custom fusion | bytes 38748200 | tf_op jit(solution)/shard_map/jit(_take)/gather | solution.py:77
  360.5 5.3 mini-gather-slice.5
  365.8 10.4 %gather_fusion.3 = bf16[10,688,1280]{2,1,0:T(8,128)(2,1)} fusion(bf16[3,688,1280]{2,1,0:T(8,128)(2,1)} %mini-gather-slice.5, s32[1024]{0:T(1024)S(1)} %pad_clamp_fusion), kind=kCustom, calls=%fused_computation.3 | custom fusion | bytes 35225640 | tf_op jit(solution)/shard_map/jit(_take)/gather | solution.py:77
  376.2 89.0 %reduce-scatter.3.cloned.1.call-done = bf16[3,688,1024]{2,1,0:T(8,128)(2,1)} async-done(((bf16[3,688,4096]{2,1,0:T(8,128)(2,1)}), bf16[3,688,1024]{2,1,0:T(8,128)(2,1)}) %reduce-scatter.3.cloned.1.call-update) | async-done | bytes 4227088 | tf_op jit(solution)/shard_map/reduce_scatter | solution.py:31
  465.3 33.9 %fusion.9 = f32[10,128,688]{2,1,0:T(8,128)} fusion(bf16[10,128,4096]{2,1,0:T(8,128)(2,1)} %bitcast.31, bf16[10,688,1280]{2,1,0:T(8,128)(2,1)} %gather_fusion.3, bf16[10,688,1408]{2,1,0:T(8,128)(2,1)} %gather_fusion.2, bf16[10,688,1408]{2,1,0:T(8,128)(2,1)} %gather_fusion.1, pred[10]{0:T(512)(128)(4,1)S(1)} %compare_and_fusion), kind=kOutput, calls=%fused_computation.19 | convolution fusion | flops 7411466240 | bytes 70369288 | tf_op jit(solution)/shard_map/bkw,bfw->bkf/dot_general | solution.py:78
  499.2 8.1 %gather_fusion = f32[1024,688]{1,0:T(8,128)} fusion(f32[1280,688]{1,0:T(8,128)} %bitcast.30, s32[1024]{0:T(1024)S(1)} %copy-done.8), kind=kCustom, calls=%fused_computation | custom fusion | bytes 5640192 | tf_op jit(solution)/shard_map/gather | solution.py:80
  507.3 5.1 multiply_convert_fusion
  512.4 2.5 copy.32
  515.0 2.5 copy.33
  517.5 7.1 %reduce-scatter.5.cloned.1.call-done = bf16[3,688,512]{2,1,0:T(8,128)(2,1)} async-done(((bf16[3,688,1024]{2,1,0:T(8,128)(2,1)}), bf16[3,688,512]{2,1,0:T(8,128)(2,1)}) %reduce-scatter.5.cloned.1.call-update) | async-done | bytes 2113552 | tf_op jit(solution)/shard_map/reduce_scatter | solution.py:31
  524.5 4.2 convert_element_type.76
  (43 shorter events, 3.1 us)
Async XLA Ops:
  7.2 64.7 %copy-start.5 = (s32[1024]{0:T(1024)S(1)}, s32[1024]{0:T(1024)}, u32[]{:S(2)}) copy-start(s32[1024]{0:T(1024)} %param.11) | copy-start | bytes 12292
  7.2 75.7 %copy-start.4 = (bf16[1024,688]{0,1:T(8,128)(2,1)S(1)}, bf16[1024,688]{0,1:T(8,128)(2,1)}, u32[]{:S(2)}) copy-start(bf16[1024,688]{0,1:T(8,128)(2,1)} %param.13) | copy-start | bytes 4227076
  7.2 64.6 %all-gather.6.cloned.1.call-start = ((), (), s32[]{:S(2)}) async-start(), calls=%async_computation.6 | async-start | bytes 6340608 | tf_op jit(solution)/shard_map/all_gather | solution.py:25
  9.3 11.5 %all-to-all-start = ((f32[8,1,3]{2,1,0:T(1,128)}), f32[8,1,3]{2,1,0:T(1,128)S(1)}, u32[]{:S(2)}, u32[]{:S(2)}) async-start(f32[8,1,3]{2,1,0:T(1,128)} %broadcast_in_dim.15), calls=%async_computation | async-start | bytes 8192 | tf_op jit(solution)/shard_map/all_to_all | solution.py:14
  14.8 137.5 %all-gather.4.cloned.1.call-start = ((), (), s32[]{:S(2)}) async-start(), calls=%async_computation.3 | async-start | bytes 8912896 | tf_op jit(solution)/shard_map/all_gather | solution.py:48
  23.8 298.0 %all-gather.8.cloned.1.call-start = ((), (), s32[]{:S(2)}) async-start(), calls=%async_computation.7 | async-start | bytes 21135360 | tf_op jit(solution)/shard_map/all_gather | solution.py:25
  71.8 393.4 %reduce-scatter.3.cloned.1.call-start = ((), (), s32[]{:S(2)}) async-start(), calls=%async_computation.4 | async-start | bytes 21135360 | tf_op jit(solution)/shard_map/reduce_scatter | solution.py:31
  83.6 88.0 %copy-start = (bf16[1024,688]{1,0:T(8,128)(2,1)}, bf16[1024,688]{1,0:T(8,128)(2,1)S(1)}, u32[]{:S(2)}) copy-start(bf16[1024,688]{1,0:T(8,128)(2,1)S(1)} %copy.28) | copy-start | bytes 4227076
  85.9 85.8 %copy-start.2 = (bf16[1024,688]{1,0:T(8,128)(2,1)}, bf16[1024,688]{1,0:T(8,128)(2,1)S(1)}, u32[]{:S(2)}) copy-start(bf16[1024,688]{1,0:T(8,128)(2,1)S(1)} %copy.29) | copy-start | bytes 4227076
  86.8 84.8 %copy-start.6 = (s32[1024,1]{0,1:T(1,128)}, s32[1024,1]{0,1:T(1,128)S(1)}, u32[]{:S(2)}) copy-start(s32[1024,1]{0,1:T(1,128)S(1)} %compare_select_fusion) | copy-start | bytes 12292
  319.6 1.6 copy-start.7
  319.6 204.9 %reduce-scatter.5.cloned.1.call-start = ((), (), s32[]{:S(2)}) async-start(), calls=%async_computation.5 | async-start | bytes 6340608 | tf_op jit(solution)/shard_map/reduce_scatter | solution.py:31
  465.3 33.9 %copy-start.8 = (s32[1024]{0:T(1024)S(1)}, s32[1024]{0:T(1024)}, u32[]{:S(2)}) copy-start(s32[1024]{0:T(1024)} %broadcast_clamp_fusion) | copy-start | bytes 12292
  499.2 8.1 %copy-start.1 = (bf16[1024,688]{1,0:T(8,128)(2,1)S(1)}, bf16[1024,688]{1,0:T(8,128)(2,1)}, u32[]{:S(2)}) copy-start(bf16[1024,688]{1,0:T(8,128)(2,1)} %copy-done) | copy-start | bytes 4227076
  499.2 8.1 %copy-start.3 = (bf16[1024,688]{1,0:T(8,128)(2,1)S(1)}, bf16[1024,688]{1,0:T(8,128)(2,1)}, u32[]{:S(2)}) copy-start(bf16[1024,688]{1,0:T(8,128)(2,1)} %copy-done.2) | copy-start | bytes 4227076
Sparse Core Ops, SparseCore 0:
  9.6 62.0 all-gather.5
  74.7 77.5 all-gather.3
  154.0 153.6 all-gather.7
  319.8 145.4 reduce-scatter.2
  467.5 56.9 reduce-scatter.4
where the time goes:
time: 538 us; the launch traced here: 535 us
  waiting for transfers between devices  209 us (39%)
  matrix products  139 us (26%)
  local copies, waits for them, and re-layouts  108 us (20%)
  other arithmetic  50.5 us (9%)
  between operations  23 us (4%)
  starting transfers between devices  5.88 us (1%)
    dot_general x10, matrix products, add_block(): lax.dot_general(rows_hidden, rows_scaled, (((0,), (0,)), ((), ())), prefe...  105 us
    reduce_scatter x2, waiting for transfers between devices, sum_by_axis(): shard = lax.psum_scatter(shard, axis, scatter_dimension=dim, tiled=True)  96.1 us
    all_gather x1, waiting for transfers between devices, shards(): scaled = lax.all_gather(scaled_part, 'tensor', axis=1, tiled=True)  58 us
    gather x5, local copies, waits for them, and re-layouts, shards(): chosen = jnp.take(weight_piece, block_kind, axis=0)  54.4 us
    all_gather x2, waiting for transfers between devices, gather_axes(): shard = lax.all_gather(shard, axis, axis=dim, tiled=True)  47.9 us
    dot_general x1, matrix products, shards(): jnp.einsum('bkw,bfw->bkf', columns, chosen, preferred_element_type=jnp.fl...  33.9 us
    another operation x3, other arithmetic, shards(): partial_sum = jnp.stack([kind_product(kind_id) for kind_id in range(3)])  26 us
    scatter x1, local copies, waits for them, and re-layouts, shards(): jnp.zeros((capacity, width_all), jnp.bfloat16).at[slot_index].set(scaled)  19.3 us
  transfers between devices with their start and end apart: 6, of which 5 were waited for; matrix products, arithmetic and copies ran while one was open for 55% of the time, Pallas kernels for 0%

commit v1 on v0

v1 whole, which is shorter than its diff:
```python
import jax
import jax.numpy as jnp
from jax import lax
from jax.experimental import pallas as pl
from jax.experimental.pallas import tpu as pltpu
from jax.sharding import Mesh
from jax.sharding import PartitionSpec as P

AXES = ("x", "yl", "z", "yh", "c")
MESH = pl.DeviceIdType.MESH
F32, BF16 = jnp.float32, jnp.bfloat16
S1, YH, ZZ, CC, WW, MM, HR, HL, HFR, HFL = 0, 4, 5, 11, 19, 22, 29, 33, 37, 41
TR, TL, DR1, DL1, DR2, DL2, DW, SEMS = 45, 49, 53, 57, 61, 65, 69, 72


def dot_nt(a, b):
    return lax.dot_general(a, b, (((1,), (1,)), ((), ())), preferred_element_type=F32)


def eye(n):
    same = lax.broadcasted_iota(jnp.int32, (n, n), 0) == lax.broadcasted_iota(jnp.int32, (n, n), 1)
    return same.astype(F32).astype(BF16)


def kernel(
    mod_ref, og_ref, gate_ref, up_ref, w_ref, dw_ref, gg_ref, ug_ref,
    s_ref, wv_ref, ht_ref, part_ref, from_left, from_right, hop_left, hop_right,
    acc_ref, out_half, in_half, gate_v, up_v, mod_all, kind_ref, eye_f, eye_q,
    send, recv, local,
):
    x, yl, z, yh, c = (lax.axis_index(a) for a in AXES)
    rows, ff = gate_ref.shape
    quarter, cols = rows // 4, og_ref.shape[1]
    half = 2 * cols
    total = rows * 8
    cut = (ff // 2 + 15) // 16 * 16
    top, low = pl.ds(0, cut), pl.ds(cut, ff - cut)
    right, left, across = (x + 1) % 4, (x + 3) % 4, (x + 2) % 4
    up_z, down_z = (z + 1) % 4, (z + 3) % 4

    def rc(src, dst, si, ri, **where):
        return pltpu.make_async_remote_copy(
            src_ref=src, dst_ref=dst, send_sem=send.at[si], recv_sem=recv.at[ri],
            device_id=where, device_id_type=MESH,
        )

    def order(k):
        return (z + 3 * k + 3 * (k // 2) + 2 * (k // 3)) % 4

    def tile(i, n):
        return pl.ds(pl.multiple_of(i * n, n), n)

    def s_block(q, e, core):
        return s_ref.at[q, :, tile(((yh + e) % 2) * 2 + core, cols)]

    def w_copy(m):
        return rc(w_ref.at[m], wv_ref.at[m, :, tile(yl, half)], WW + m, WW + m, yl=1 - yl)

    def w_local(m):
        return pltpu.make_async_copy(w_ref.at[m], wv_ref.at[m, :, tile(yl, half)], local.at[2 + m])

    def first_dst(q, source):
        return s_ref.at[q, tile(source, quarter), tile(yh * 2 + c, cols)]

    def first_remote(q):
        return rc(og_ref.at[tile(q, quarter), :], first_dst(q, x), S1 + q, S1 + x, x=z, z=q)

    def is_self(q):
        return jnp.logical_and(x == z, q == z)

    for q in range(4):
        @pl.when(jnp.logical_not(is_self(q)))
        def _():
            first_remote(q).start()

        @pl.when(is_self(q))
        def _():
            pltpu.make_async_copy(
                og_ref.at[tile(q, quarter), :], first_dst(q, x), recv.at[S1 + x]
            ).start()

    w_copy(0).start()
    loads = [
        pltpu.make_async_copy(gate_ref, gate_v, local.at[0]),
        pltpu.make_async_copy(up_ref, up_v, local.at[1]),
    ]
    for copy in loads:
        copy.start()
    for m in range(3):
        w_local(m).start()
    group = x * 2 + yl
    kinds = []
    for step in range(1, 8):
        dx, dy = step // 2, step % 2
        kinds.append(
            rc(mod_ref, mod_all.at[group], MM + step - 1, MM + step - 1,
               x=(x + dx) % 4, yl=(yl + dy) % 2)
        )
    for copy in kinds:
        copy.start()
    mod_all[group] = mod_ref[...]
    eye_f[...] = eye(ff)
    eye_q[...] = eye(quarter)
    for copy in loads:
        copy.wait()

    def h_block(q, source):
        return ht_ref.at[q, :, tile(source, quarter)]

    def h_right(k):
        return rc(h_block(order(k), x), h_block(order(k), x), HR + k, HR + k, x=right)

    def h_left(k):
        return rc(h_block(order(k), x), h_block(order(k), x), HL + k, HL + k, x=left)

    def h_on_right(k):
        block = ht_ref.at[order(k), top, tile(left, quarter)]
        return rc(block, block, HFR + k, HFR + k, x=right)

    def h_on_left(k):
        block = ht_ref.at[order(k), low, tile(right, quarter)]
        return rc(block, block, HFL + k, HFL + k, x=left)

    def make_hidden(k, _):
        q = order(k)
        g = gate_v[tile(q, quarter), :].astype(F32)
        u = up_v[tile(q, quarter), :].astype(F32)
        hidden = (g * jax.nn.sigmoid(g) * u).astype(BF16)
        ht_ref[q, :, tile(x, quarter)] = dot_nt(eye_f[...], hidden).astype(BF16)
        h_right(k).start()
        h_left(k).start()
        return 0

    lax.fori_loop(0, 4, make_hidden, 0)

    def first_in(source):
        dst = first_dst(z, source)
        return rc(dst, dst, S1, S1 + source, x=right)

    def swap(e):
        block = s_block(z, e, c)
        return rc(block, block, YH, YH, yh=1 - yh)

    def ring(q, e, i, to):
        block = s_block(q, e, c)
        return rc(block, block, ZZ + i, ZZ + i, z=to)

    def share(k, e, core):
        block = s_block(order(k), e, core)
        return rc(block, block, CC + 2 * k + e, CC + 2 * k + e, c=1 - c)

    for source in range(4):
        first_in(source).wait_recv()
    swap(0).start()
    ring(z, 0, 0, up_z).start()
    ring(z, 0, 2, down_z).start()
    share(0, 0, c).start()
    w_copy(1).start()
    w_copy(2).start()

    def pass_hidden(k, _):
        q = order(k)
        a = h_block(q, left)
        rc(a, a, HR + k, HR + k, x=right).wait_recv()
        h_on_right(k).start()
        b = h_block(q, right)
        rc(b, b, HL + k, HL + k, x=left).wait_recv()
        h_on_left(k).start()
        return 0

    lax.fori_loop(0, 2, pass_hidden, 0)
    ring(down_z, 0, 0, up_z).wait_recv()
    ring(down_z, 0, 4, up_z).start()
    share(1, 0, c).start()
    ring(up_z, 0, 2, down_z).wait_recv()
    share(2, 0, c).start()
    swap(1).wait_recv()
    ring(z, 1, 1, up_z).start()
    ring(z, 1, 3, down_z).start()
    share(0, 1, c).start()
    lax.fori_loop(2, 4, pass_hidden, 0)
    ring(up_z, 1, 3, down_z).wait_recv()
    ring(up_z, 1, 5, down_z).start()
    share(2, 1, c).start()
    ring(down_z, 1, 1, up_z).wait_recv()
    share(1, 1, c).start()
    far = (z + 2) % 4
    ring(far, 0, 4, up_z).wait_recv()
    share(3, 0, c).start()
    ring(far, 1, 5, down_z).wait_recv()
    share(3, 1, c).start()

    for step in range(1, 8):
        dx, dy = step // 2, step % 2
        source = ((x + 4 - dx) % 4) * 2 + (yl + dy) % 2
        rc(mod_ref, mod_all.at[source], MM, MM + step - 1, x=right).wait_recv()
    for q in range(4):
        pieces = []
        for source in range(4):
            one = mod_all[source * 2 + yl]
            pieces += [one[2 * q : 2 * q + 1, :], one[2 * q + 1 : 2 * q + 2, :]]
        kind_ref[q] = jnp.concatenate(pieces, axis=1)
    everyone = mod_all[...].reshape(rows // 128 * 8, 128)
    factors = []
    for m in range(3):
        hits = (everyone == m).astype(F32)
        count = jnp.sum(jnp.sum(hits, axis=0, keepdims=True), axis=1, keepdims=True)
        factors.append(total / (3.0 * count))

    for m in range(3):
        w_local(m).wait()
        theirs = wv_ref.at[m, :, tile(1 - yl, half)]
        rc(theirs, theirs, WW + m, WW + m, yl=1 - yl).wait_recv()

    def hop(k, to_right):
        q = order(k)
        if to_right:
            return rc(part_ref.at[across, q, top, :], hop_left.at[k], TR + k, TR + k, x=right)
        return rc(part_ref.at[across, q, low, :], hop_right.at[k], TL + k, TL + k, x=left)

    def give(k, to_right, rows_at, base):
        q = order(k)
        if to_right:
            return rc(part_ref.at[right, q, rows_at, :], from_left.at[k, rows_at, :],
                      base + k, base + k, x=right)
        return rc(part_ref.at[left, q, rows_at, :], from_right.at[k, rows_at, :],
                  base + k, base + k, x=left)

    def gives(k, i):
        return give(k, i % 2 == 0, (low, top, top, low)[i], (DR1, DL1, DR2, DL2)[i])

    def relay(k):
        q = order(k)
        hop(k, True).wait_recv()
        part_ref[right, q, top, :] = (
            part_ref[right, q, top, :].astype(F32) + hop_left[k].astype(F32)
        ).astype(BF16)
        gives(k, 2).start()
        hop(k, False).wait_recv()
        part_ref[left, q, low, :] = (
            part_ref[left, q, low, :].astype(F32) + hop_right[k].astype(F32)
        ).astype(BF16)
        gives(k, 3).start()

    def share_in(k, e):
        share(k, e, 1 - c).wait_recv()

    def hidden_step(k, _):
        q = order(k)
        share_in(k, 0)
        share_in(k, 1)

        def pair(p, _):
            block = s_ref[q, tile(p, half), :]
            kind = kind_ref[q, :, tile(p, half)]
            got = dot_nt(wv_ref[0], block)
            for m in range(1, 3):
                got = jnp.where(kind == m, dot_nt(wv_ref[m], block), got)
            got = got.astype(BF16)
            part_ref[2 * p, q] = got[:, :quarter]
            part_ref[2 * p + 1, q] = got[:, quarter:]
            return 0

        lax.fori_loop(0, 2, pair, 0)
        hop(k, True).start()
        hop(k, False).start()
        gives(k, 0).start()
        gives(k, 1).start()

        @pl.when(k > 0)
        def _():
            relay(k - 1)

        return 0

    lax.fori_loop(0, 4, hidden_step, 0)

    def hidden_in(k, _):
        a = ht_ref.at[order(k), top, tile(across, quarter)]
        rc(a, a, HFR + k, HFR + k, x=right).wait_recv()
        b = ht_ref.at[order(k), low, tile(across, quarter)]
        rc(b, b, HFL + k, HFL + k, x=left).wait_recv()
        return 0

    lax.fori_loop(0, 4, hidden_in, 0)

    def weight_sum(m, side, dst):
        dst[...] = jnp.zeros(dst.shape, F32)

        def add(q, _):
            mark = (kind_ref[q] == m).astype(F32).astype(BF16)
            dst[...] += jnp.dot(
                ht_ref[q] * mark, s_ref[q, :, tile(side, half)], preferred_element_type=F32
            )
            return 0

        lax.fori_loop(0, 4, add, 0)

    def dw_copy(m):
        return rc(out_half.at[m], in_half.at[m], DW + m, DW + m, yl=1 - yl)

    def other_half(m, _):
        weight_sum(m, 1 - yl, acc_ref)
        out_half[m] = acc_ref[...].astype(BF16)
        dw_copy(m).start()

        @pl.when(m == 0)
        def _():
            relay(3)

        return 0

    lax.fori_loop(0, 3, other_half, 0)

    def own_half(m, _):
        weight_sum(m, yl, dw_ref.at[m])
        return 0

    lax.fori_loop(0, 3, own_half, 0)

    def finish(k, _):
        q = order(k)
        for i in range(4):
            gives(k, i).wait_recv()
        kind = kind_ref[q, :, tile(x, quarter)]
        scale = jnp.where(kind == 0, factors[0], jnp.where(kind == 1, factors[1], factors[2]))
        t = (
            part_ref[x, q].astype(F32) + from_left[k].astype(F32) + from_right[k].astype(F32)
        ) * scale
        high = t.astype(BF16)
        rest = (t - high.astype(F32)).astype(BF16)
        d = dot_nt(eye_q[...], high) + dot_nt(eye_q[...], rest)
        g = gate_v[tile(q, quarter), :].astype(F32)
        u = up_v[tile(q, quarter), :].astype(F32)
        s = jax.nn.sigmoid(g)
        ug_ref[tile(q, quarter), :] = (d * (g * s)).astype(BF16)
        gg_ref[tile(q, quarter), :] = (d * u * (s * (1.0 + g * (1.0 - s)))).astype(BF16)
        return 0

    lax.fori_loop(0, 4, finish, 0)
    for m in range(3):
        dw_copy(m).wait_recv()
        dw_ref[m] = (dw_ref[m] + in_half[m].astype(F32)) * factors[m]

    for q in range(4):
        @pl.when(jnp.logical_not(is_self(q)))
        def _():
            first_remote(q).wait_send()

    for copy in kinds:
        copy.wait_send()
    swap(0).wait_send()
    for q, e, i, to in (
        (z, 0, 0, up_z), (z, 1, 1, up_z), (z, 0, 2, down_z),
        (z, 1, 3, down_z), (down_z, 0, 4, up_z), (up_z, 1, 5, down_z),
    ):
        ring(q, e, i, to).wait_send()

    def drain(k, _):
        for copy in (h_right(k), h_left(k), h_on_right(k), h_on_left(k)):
            copy.wait_send()
        for copy in (share(k, 0, c), share(k, 1, c), hop(k, True), hop(k, False)):
            copy.wait_send()
        for i in range(4):
            gives(k, i).wait_send()
        return 0

    lax.fori_loop(0, 4, drain, 0)
    for m in range(3):
        w_copy(m).wait_send()
        dw_copy(m).wait_send()


def shards(modality, out_grad, gate_pre, up_pre, down_weight):
    rows, cols = out_grad.shape
    kinds, ff, half = down_weight.shape
    quarter = rows // 4
    cut = (ff // 2 + 15) // 16 * 16
    anywhere = pl.BlockSpec(memory_space=pl.ANY)
    vmem = pl.BlockSpec(memory_space=pltpu.VMEM)
    return pl.pallas_call(
        kernel,
        out_shape=(
            jax.ShapeDtypeStruct((kinds, ff, half), F32),
            jax.ShapeDtypeStruct((rows, ff), BF16),
            jax.ShapeDtypeStruct((rows, ff), BF16),
        ),
        in_specs=[vmem, anywhere, anywhere, anywhere, anywhere],
        out_specs=(vmem, vmem, vmem),
        scratch_shapes=[
            pltpu.VMEM((4, rows, 4 * cols), BF16),
            pltpu.VMEM((kinds, ff, 2 * half), BF16),
            pltpu.VMEM((4, ff, rows), BF16),
            pltpu.VMEM((4, 4, ff, quarter), BF16),
            pltpu.VMEM((4, ff, quarter), BF16),
            pltpu.VMEM((4, ff, quarter), BF16),
            pltpu.VMEM((4, cut, quarter), BF16),
            pltpu.VMEM((4, ff - cut, quarter), BF16),
            pltpu.VMEM((ff, half), F32),
            pltpu.VMEM((kinds, ff, half), BF16),
            pltpu.VMEM((kinds, ff, half), BF16),
            pltpu.VMEM((rows, ff), BF16),
            pltpu.VMEM((rows, ff), BF16),
            pltpu.VMEM((8, rows // 128, 128), jnp.int32),
            pltpu.VMEM((4, 1, rows), jnp.int32),
            pltpu.VMEM((ff, ff), BF16),
            pltpu.VMEM((quarter, quarter), BF16),
            pltpu.SemaphoreType.DMA((SEMS,)),
            pltpu.SemaphoreType.DMA((SEMS,)),
            pltpu.SemaphoreType.DMA((5,)),
        ],
        compiler_params=pltpu.CompilerParams(
            has_side_effects=True, vmem_limit_bytes=67_000_000
        ),
    )(modality.reshape(rows // 128, 128), out_grad, gate_pre, up_pre, down_weight)


def solution(mesh):
    torus = Mesh(mesh.devices.reshape(4, 2, 4, 2, 2), AXES)
    fsdp, tensor = ("x", "yl"), ("z", "yh", "c")
    in_specs = (
        P(fsdp),
        P(fsdp, tensor),
        P(fsdp, tensor),
        P(fsdp, tensor),
        P(None, tensor, fsdp),
    )
    out_specs = (P(None, tensor, fsdp), P(fsdp, tensor), P(fsdp, tensor))
    return jax.shard_map(
        shards, mesh=torus, in_specs=in_specs, out_specs=out_specs, check_vma=False
    )
```

time: 538 us -> 178 us (0.33)
  waiting for transfers between devices: 209 us -> 0 us
  Pallas kernels: 0 us -> 162 us
  matrix products: 139 us -> 0 us
  local copies, waits for them, and re-layouts: 108 us -> 13 us
  other arithmetic: 50.5 us -> 0 us
  between operations: 23 us -> 0.66 us
  starting transfers between devices: 5.88 us -> 0 us
    pallas_call x0 -> x1, Pallas kernels: none -> 162 us  [shards(): pl.pallas_call(kernel, out_shape=(jax.ShapeDtypeStruct((kinds, ff, half),...]
    dot_general x11 -> x0, matrix products: 139 us -> none  [the longest x10 105 us: add_block(): lax.dot_general(rows_hidden, rows_scaled, (((0,), (0,)), ((), ())), prefe...]
    all_gather x3 -> x0, waiting for transfers between devices: 106 us -> none  [the longest x1 58 us: shards(): scaled = lax.all_gather(scaled_part, 'tensor', axis=1, tiled=True)]
    reduce_scatter x2 -> x0, waiting for transfers between devices: 96.1 us -> none  [sum_by_axis(): shard = lax.psum_scatter(shard, axis, scatter_dimension=dim, tiled=True)]
    gather x6 -> x0, local copies, waits for them, and re-layouts: 62.5 us -> none  [the longest x5 54.4 us: shards(): chosen = jnp.take(weight_piece, block_kind, axis=0)]
    another operation x6 -> x0, other arithmetic: 27.8 us -> none  [the longest x3 26 us: shards(): partial_sum = jnp.stack([kind_product(kind_id) for kind_id in range(3)])]
    scatter x1 -> x0, local copies, waits for them, and re-layouts: 19.3 us -> none  [shards(): jnp.zeros((capacity, width_all), jnp.bfloat16).at[slot_index].set(scaled)]
    another operation x3 -> x0, local copies, waits for them, and re-layouts: 16.8 us -> none
  transfers between devices with their start and end apart: 6 -> 0, of which waited for: 5 -> 0; matrix products, arithmetic and copies ran while one was open for 55% -> 0% of each run, Pallas kernels for 0% -> 0%
where the time goes in v1:
time: 178 us; the launch traced here: 176 us
  Pallas kernels  162 us (91%)
  local copies, waits for them, and re-layouts  13 us (7%)
    pallas_call x1, Pallas kernels, shards(): pl.pallas_call(kernel, out_shape=(jax.ShapeDtypeStruct((kinds, ff, half),...  162 us
    unnamed x7, local copies, waits for them, and re-layouts  8.9 us
    pallas_call x2, local copies, waits for them, and re-layouts, shards(): pl.pallas_call(kernel, out_shape=(jax.ShapeDtypeStruct((kinds, ff, half),...  4.14 us

profile of v1, /device:TPU:0, one launch (start us, length us, event | category | flops | bytes accessed | tf_op | source)
XLA Modules:
  0.0 175.8 jit_solution(8322190342976096418)
XLA Ops:
  0.6 0.0 copy-start.1
  0.6 2.7 %copy.8.gate_ref = bf16[1024,688]{1,0:T(8,128)(2,1)} copy(bf16[1024,688]{0,1:T(8,128)(2,1)} %param.7) | data formatting | bytes 2818048 | tf_op args[2]
  3.3 0.0 copy-done.1
  3.3 1.6 copy.9.up_ref
  4.9 162.1 %shard_map.76 = (f32[3,688,512]{2,1,0:T(8,128)}, bf16[1024,688]{1,0:T(8,128)(2,1)}, bf16[1024,688]{1,0:T(8,128)(2,1)}) custom-call(s32[8,128]{1,0:T(8,128)} %bitcast.1, bf16[1024,256]{1,0:T(8,128)(2,1)} %og_ref.1, bf16[1024,688]{1,0:T(8,128)(2,1)} %copy.8.gate_ref, bf16[1024,688]{1,0:T(8,128)(2,1)} %copy.9.up_ref, bf16[3,688,512]{2,1,0:T(8,128)(2,1)} %w_ref.1), custom_call_target="tpu_custom_call" | custom-call | tf_op jit(solution)/shard_map/pallas_call | solution.py:381
  167.0 0.0 copy-start
  167.0 2.6 %copy.10 = bf16[1024,688]{0,1:T(8,128)(2,1)} copy(bf16[1024,688]{1,0:T(8,128)(2,1)} %get-tuple-element.4) | data formatting | bytes 2818048 | tf_op jit(solution)/shard_map/pallas_call | solution.py:381
  169.7 0.0 copy-done
  169.7 1.5 copy.11
  171.2 4.7 %copy.13 = f32[3,688,512]{2,1,0:T(8,128)} copy(f32[3,688,512]{2,1,0:T(8,128)} %get-tuple-element.9) | data formatting | bytes 8454144
Async XLA Ops:
  0.6 2.7 %copy-start.1 = (bf16[1024,688]{0,1:T(8,128)(2,1)S(1)}, bf16[1024,688]{0,1:T(8,128)(2,1)}, u32[]{:S(2)}) copy-start(bf16[1024,688]{0,1:T(8,128)(2,1)} %param.8) | copy-start | bytes 4227076
  167.0 2.6 %copy-start = (bf16[1024,688]{1,0:T(8,128)(2,1)S(1)}, bf16[1024,688]{1,0:T(8,128)(2,1)}, u32[]{:S(2)}) copy-start(bf16[1024,688]{1,0:T(8,128)(2,1)} %get-tuple-element.5) | copy-start | bytes 4227076

commit v2 on v1

v2 whole, which is shorter than its diff:
```python
import jax
import jax.numpy as jnp
from jax import lax
from jax.experimental import pallas as pl
from jax.experimental.pallas import tpu as pltpu
from jax.sharding import Mesh
from jax.sharding import PartitionSpec as P

AXES = ("x", "yl", "z", "yh", "c")
MESH = pl.DeviceIdType.MESH
F32, BF16 = jnp.float32, jnp.bfloat16
S1, Z1, YH, UP0, UP1, DN0, DN1, FUP, FDN, CC = 0, 4, 8, 12, 16, 20, 24, 28, 32, 36
WW, MM, HR, HL, HFR, HFL = 68, 71, 78, 82, 86, 90
TR, TL, DR1, DL1, DR2, DL2, DW, SEMS = 94, 98, 102, 106, 110, 114, 118, 121


def dot_nt(a, b):
    return lax.dot_general(a, b, (((1,), (1,)), ((), ())), preferred_element_type=F32)


def kernel(
    mod_ref, og_ref, gate_ref, up_ref, w_ref, own_ref, theirs_ref, factor_ref, gg_ref, ug_ref,
    zin_ref, s_ref, wv_ref, ht_ref, part_ref, from_left, from_right, hop_left, hop_right,
    acc_ref, own_v, out_half, gate_v, up_v, mod_all, kind_ref,
    send, recv, local,
):
    x, yl, z, yh, c = (lax.axis_index(a) for a in AXES)
    ff, rows = gate_ref.shape
    quarter, cols = rows // 4, og_ref.shape[1]
    half = 2 * cols
    total = rows * 8
    cut = (ff // 2 + 15) // 16 * 16
    top, low = pl.ds(0, cut), pl.ds(cut, ff - cut)
    right, left, across = (x + 1) % 4, (x + 3) % 4, (x + 2) % 4
    up_z, down_z = (z + 1) % 4, (z + 3) % 4
    diagonal = x == z

    barrier = pltpu.get_barrier_semaphore()
    group_steps = [(s // 2, s % 2) for s in range(1, 8)]
    for dx, dy in group_steps:
        pl.semaphore_signal(
            barrier, inc=1, device_id={"x": (x + dx) % 4, "yl": (yl + dy) % 2}, device_id_type=MESH
        )
    for d in range(1, 4):
        pl.semaphore_signal(barrier, inc=1, device_id={"z": (z + d) % 4}, device_id_type=MESH)
    pl.semaphore_signal(barrier, inc=1, device_id={"yh": 1 - yh}, device_id_type=MESH)
    pl.semaphore_signal(barrier, inc=1, device_id={"c": 1 - c}, device_id_type=MESH)

    def rc(src, dst, si, ri, **where):
        return pltpu.make_async_remote_copy(
            src_ref=src, dst_ref=dst, send_sem=send.at[si], recv_sem=recv.at[ri],
            device_id=where, device_id_type=MESH,
        )

    def turn(i):
        return 3 * i + 3 * (i // 2) + 2 * (i // 3)

    def order(k):
        return (z + turn(k)) % 4

    def source(j):
        return (x + turn(j)) % 4

    def tile(i, n):
        return pl.ds(pl.multiple_of(i * n, n), n)

    def each(n, body, start=0):
        def step(i, _):
            body(i)
            return 0

        lax.fori_loop(start, n, step, 0)

    loads = [
        pltpu.make_async_copy(gate_ref, gate_v, local.at[0]),
        pltpu.make_async_copy(up_ref, up_v, local.at[1]),
    ]
    for copy in loads:
        copy.start()

    def w_copy(m):
        return rc(w_ref.at[m], wv_ref.at[m, :, tile(yl, half)], WW + m, WW + m, yl=1 - yl)

    def w_local(m):
        return pltpu.make_async_copy(w_ref.at[m], wv_ref.at[m, :, tile(yl, half)], local.at[2 + m])

    for m in range(3):
        w_local(m).start()
    group = x * 2 + yl
    mod_all[group] = mod_ref[...]
    for copy in loads:
        copy.wait()

    def make_hidden(k):
        q = order(k)
        g = gate_v[:, tile(q, quarter)].astype(F32)
        u = up_v[:, tile(q, quarter)].astype(F32)
        ht_ref[q, :, tile(x, quarter)] = (g * jax.nn.sigmoid(g) * u).astype(BF16)

    each(1, make_hidden)
    pl.semaphore_wait(barrier, 12)

    def s_first(q, src):
        return s_ref.at[q, tile(src, quarter), tile(yh * 2 + c, cols)]

    def along_z(d, direct):
        q = (z + d) % 4
        src = og_ref.at[tile(q, quarter), :]
        if direct:
            return rc(src, s_first(q, x), Z1 + d, S1 + x, z=q)
        return rc(src, zin_ref.at[d], Z1 + d, Z1 + d, z=q)

    def home():
        return rc(og_ref.at[tile(z, quarter), :], s_first(z, x), Z1, S1 + x, x=z)

    def along_x(d):
        return rc(zin_ref.at[d], s_first(z, x), S1 + d, S1 + x, x=(z + 4 - d) % 4)

    def passes(d):
        return (z + 4 - d) % 4 != x

    @pl.when(diagonal)
    def _():
        for d in (1, 3, 2):
            along_z(d, True).start()
        pltpu.make_async_copy(
            og_ref.at[tile(z, quarter), :], s_first(z, x), recv.at[S1 + x]
        ).start()

    @pl.when(jnp.logical_not(diagonal))
    def _():
        for d in (1, 3, 2):
            along_z(d, False).start()
        home().start()

    w_copy(0).start()

    def kinds_copy(i):
        dx, dy = group_steps[i]
        return rc(mod_ref, mod_all.at[group], MM + i, MM + i, x=(x + dx) % 4, yl=(yl + dy) % 2)

    for i in range(7):
        kinds_copy(i).start()

    def h_block(q, src):
        return ht_ref.at[q, :, tile(src, quarter)]

    def h_right(k):
        return rc(h_block(order(k), x), h_block(order(k), x), HR + k, HR + k, x=right)

    def h_left(k):
        return rc(h_block(order(k), x), h_block(order(k), x), HL + k, HL + k, x=left)

    def h_on_right(k):
        block = ht_ref.at[order(k), top, tile(left, quarter)]
        return rc(block, block, HFR + k, HFR + k, x=right)

    def h_on_left(k):
        block = ht_ref.at[order(k), low, tile(right, quarter)]
        return rc(block, block, HFL + k, HFL + k, x=left)

    def send_hidden(k):
        h_right(k).start()
        h_left(k).start()

    send_hidden(0)
    each(4, make_hidden, 1)
    acc_ref[...] = jnp.zeros(acc_ref.shape, F32)

    for d in (1, 3, 2):
        @pl.when(passes(d))
        def _():
            rc(zin_ref.at[d], zin_ref.at[d], Z1 + d, Z1 + d, z=z).wait_recv()
            along_x(d).start()

    each(4, send_hidden, 1)

    def piece(q, e, core, j):
        return s_ref.at[q, tile(source(j), quarter), tile(((yh + e) % 2) * 2 + core, cols)]

    def swap(e, j):
        return rc(piece(z, e, c, j), piece(z, e, c, j), YH + j, YH + j, yh=1 - yh)

    def ring(q, e, j, base, to):
        return rc(piece(q, e, c, j), piece(q, e, c, j), base + j, base + j, z=to)

    def share(k, e, j, core):
        i = CC + 8 * k + 4 * e + j
        return rc(piece(order(k), e, core, j), piece(order(k), e, core, j), i, i, c=1 - c)

    def spread_own(j):
        dst = s_first(z, source(j))
        rc(dst, dst, S1, S1 + source(j), x=right).wait_recv()
        swap(0, j).start()
        ring(z, 0, j, UP0, up_z).start()
        ring(z, 0, j, DN0, down_z).start()
        share(0, 0, j, c).start()

    each(4, spread_own)
    w_copy(1).start()
    w_copy(2).start()

    def pass_hidden(k):
        q = order(k)
        rc(h_block(q, left), h_block(q, left), HR + k, HR + k, x=right).wait_recv()
        h_on_right(k).start()
        rc(h_block(q, right), h_block(q, right), HL + k, HL + k, x=left).wait_recv()
        h_on_left(k).start()

    each(1, pass_hidden)

    def spread_other(j):
        swap(1, j).wait_recv()
        ring(z, 1, j, UP1, up_z).start()
        ring(z, 1, j, DN1, down_z).start()
        share(0, 1, j, c).start()
        ring(down_z, 0, j, UP0, up_z).wait_recv()
        ring(down_z, 0, j, FUP, up_z).start()
        share(1, 0, j, c).start()
        ring(up_z, 0, j, DN0, down_z).wait_recv()
        share(2, 0, j, c).start()

    each(4, spread_other)
    each(3, pass_hidden, 1)

    for i in range(7):
        dx, dy = group_steps[i]
        src = ((x + 4 - dx) % 4) * 2 + (yl + dy) % 2
        rc(mod_ref, mod_all.at[src], MM, MM + i, x=right).wait_recv()
    for q in range(4):
        pieces = []
        for src in range(4):
            one = mod_all[src * 2 + yl]
            pieces += [one[2 * q : 2 * q + 1, :], one[2 * q + 1 : 2 * q + 2, :]]
        kind_ref[q] = jnp.concatenate(pieces, axis=1)
    everyone = mod_all[...].reshape(rows // 128 * 8, 128)
    factors = []
    for m in range(3):
        hits = (everyone == m).astype(F32)
        count = jnp.sum(jnp.sum(hits, axis=0, keepdims=True), axis=1, keepdims=True)
        factors.append(total / (3.0 * count))
        factor_ref[m : m + 1, :] = jnp.broadcast_to(factors[m], (1, 128))

    def block_in(k):
        def one(i):
            share(k, i // 4, i % 4, 1 - c).wait_recv()

        each(8, one)

    def hidden_in(k):
        q = order(k)
        a = ht_ref.at[q, top, tile(across, quarter)]
        rc(a, a, HFR + k, HFR + k, x=right).wait_recv()
        b = ht_ref.at[q, low, tile(across, quarter)]
        rc(b, b, HFL + k, HFL + k, x=left).wait_recv()

    def marked(q, m):
        return ht_ref[q] * (kind_ref[q] == m).astype(F32).astype(BF16)

    def add_quarter(k):
        q = order(k)
        block_in(k)
        hidden_in(k)

        def one(m):
            acc_ref[m] += jnp.dot(marked(q, m), s_ref[q], preferred_element_type=F32)

        each(3, one)

    def spread_near(j):
        ring(up_z, 1, j, DN1, down_z).wait_recv()
        ring(up_z, 1, j, FDN, down_z).start()
        share(2, 1, j, c).start()
        ring(down_z, 1, j, UP1, up_z).wait_recv()
        share(1, 1, j, c).start()

    far = (z + 2) % 4

    def spread_far(j):
        ring(far, 0, j, FUP, up_z).wait_recv()
        share(3, 0, j, c).start()
        ring(far, 1, j, FDN, down_z).wait_recv()
        share(3, 1, j, c).start()

    each(4, spread_near)
    each(4, pass_hidden, 3)
    each(2, add_quarter)
    each(4, spread_far)
    each(3, add_quarter, 2)
    for m in range(3):
        w_local(m).wait()
        theirs = wv_ref.at[m, :, tile(1 - yl, half)]
        rc(theirs, theirs, WW + m, WW + m, yl=1 - yl).wait_recv()

    def hop(k, to_right):
        q = order(k)
        if to_right:
            return rc(part_ref.at[across, q, top, :], hop_left.at[k], TR + k, TR + k, x=right)
        return rc(part_ref.at[across, q, low, :], hop_right.at[k], TL + k, TL + k, x=left)

    def give(k, to_right, rows_at, base):
        q = order(k)
        if to_right:
            return rc(part_ref.at[right, q, rows_at, :], from_left.at[k, rows_at, :],
                      base + k, base + k, x=right)
        return rc(part_ref.at[left, q, rows_at, :], from_right.at[k, rows_at, :],
                  base + k, base + k, x=left)

    def gives(k, i):
        return give(k, i % 2 == 0, (low, top, top, low)[i], (DR1, DL1, DR2, DL2)[i])

    def relay(k):
        q = order(k)
        hop(k, True).wait_recv()
        part_ref[right, q, top, :] = (
            part_ref[right, q, top, :].astype(F32) + hop_left[k].astype(F32)
        ).astype(BF16)
        gives(k, 2).start()
        hop(k, False).wait_recv()
        part_ref[left, q, low, :] = (
            part_ref[left, q, low, :].astype(F32) + hop_right[k].astype(F32)
        ).astype(BF16)
        gives(k, 3).start()

    def d_hidden(k):
        q = order(k)

        def pair(p):
            block = s_ref[q, tile(p, half), :]
            kind = kind_ref[q, :, tile(p, half)]
            got = dot_nt(wv_ref[0], block)
            for m in range(1, 3):
                got = jnp.where(kind == m, dot_nt(wv_ref[m], block), got)
            got = got.astype(BF16)
            part_ref[2 * p, q] = got[:, :quarter]
            part_ref[2 * p + 1, q] = got[:, quarter:]

        each(2, pair)
        hop(k, True).start()
        hop(k, False).start()
        gives(k, 0).start()
        gives(k, 1).start()

    def dw_copy(m):
        return rc(out_half.at[m], theirs_ref.at[m], DW + m, DW + m, yl=1 - yl)

    def own_out(m):
        return pltpu.make_async_copy(own_v.at[m], own_ref.at[m], local.at[5 + m])

    def last_sum(m, side):
        q = order(3)
        at = tile(side, half)
        return acc_ref[m, :, at] + jnp.dot(
            marked(q, m), s_ref[q, :, at], preferred_element_type=F32
        )

    def other_half(m):
        out_half[m] = last_sum(m, 1 - yl).astype(BF16)
        dw_copy(m).start()

    def own_half(m):
        own_v[m] = last_sum(m, yl).astype(BF16)
        own_out(m).start()

    d_hidden(0)
    block_in(3)
    hidden_in(3)
    each(3, other_half)

    def more_d_hidden(k):
        d_hidden(k)
        relay(k - 1)

    each(4, more_d_hidden, 1)
    each(3, own_half)
    relay(3)

    def grads_out(k):
        at = tile(order(k), quarter)
        return (
            pltpu.make_async_copy(up_v.at[:, at], ug_ref.at[:, at], local.at[8 + k]),
            pltpu.make_async_copy(gate_v.at[:, at], gg_ref.at[:, at], local.at[12 + k]),
        )

    def finish(k):
        q = order(k)
        for i in range(4):
            gives(k, i).wait_recv()
        kind = kind_ref[q, :, tile(x, quarter)]
        scale = jnp.where(kind == 0, factors[0], jnp.where(kind == 1, factors[1], factors[2]))
        t = scale * (
            part_ref[x, q].astype(F32) + from_left[k].astype(F32) + from_right[k].astype(F32)
        )
        g = gate_v[:, tile(q, quarter)].astype(F32)
        u = up_v[:, tile(q, quarter)].astype(F32)
        s = jax.nn.sigmoid(g)
        up_v[:, tile(q, quarter)] = (t * (g * s)).astype(BF16)
        gate_v[:, tile(q, quarter)] = (t * u * (s * (1.0 + g * (1.0 - s)))).astype(BF16)
        for copy in grads_out(k):
            copy.start()

    each(4, finish)
    for m in range(3):
        own_out(m).wait()
        dw_copy(m).wait_recv()

    @pl.when(diagonal)
    def _():
        for d in range(1, 4):
            along_z(d, True).wait_send()

    @pl.when(jnp.logical_not(diagonal))
    def _():
        for d in range(1, 4):
            along_z(d, False).wait_send()
        home().wait_send()

    for d in range(1, 4):
        @pl.when(passes(d))
        def _():
            along_x(d).wait_send()

    for i in range(7):
        kinds_copy(i).wait_send()

    def drain(k):
        for copy in grads_out(k):
            copy.wait()
        swap(0, k).wait_send()
        for q, e, base, to in (
            (z, 0, UP0, up_z), (z, 1, UP1, up_z), (z, 0, DN0, down_z),
            (z, 1, DN1, down_z), (down_z, 0, FUP, up_z), (up_z, 1, FDN, down_z),
        ):
            ring(q, e, k, base, to).wait_send()
        for copy in (h_right(k), h_left(k), h_on_right(k), h_on_left(k)):
            copy.wait_send()
        for i in range(8):
            share(k, i // 4, i % 4, c).wait_send()
        for copy in (hop(k, True), hop(k, False)):
            copy.wait_send()
        for i in range(4):
            gives(k, i).wait_send()

    each(4, drain)
    for m in range(3):
        w_copy(m).wait_send()
        dw_copy(m).wait_send()


def shards(modality, out_grad, gate_pre, up_pre, down_weight):
    rows, cols = out_grad.shape
    kinds, ff, half = down_weight.shape
    quarter = rows // 4
    cut = (ff // 2 + 15) // 16 * 16
    anywhere = pl.BlockSpec(memory_space=pl.ANY)
    vmem = pl.BlockSpec(memory_space=pltpu.VMEM)
    own, theirs, factor, gate_grad, up_grad = pl.pallas_call(
        kernel,
        out_shape=(
            jax.ShapeDtypeStruct((kinds, ff, half), BF16),
            jax.ShapeDtypeStruct((kinds, ff, half), BF16),
            jax.ShapeDtypeStruct((kinds, 128), F32),
            jax.ShapeDtypeStruct((ff, rows), BF16),
            jax.ShapeDtypeStruct((ff, rows), BF16),
        ),
        in_specs=[vmem, anywhere, anywhere, anywhere, anywhere],
        out_specs=(anywhere, anywhere, vmem, anywhere, anywhere),
        scratch_shapes=[
            pltpu.VMEM((4, quarter, cols), BF16),
            pltpu.VMEM((4, rows, 4 * cols), BF16),
            pltpu.VMEM((kinds, ff, 2 * half), BF16),
            pltpu.VMEM((4, ff, rows), BF16),
            pltpu.VMEM((4, 4, ff, quarter), BF16),
            pltpu.VMEM((4, ff, quarter), BF16),
            pltpu.VMEM((4, ff, quarter), BF16),
            pltpu.VMEM((4, cut, quarter), BF16),
            pltpu.VMEM((4, ff - cut, quarter), BF16),
            pltpu.VMEM((kinds, ff, 2 * half), F32),
            pltpu.VMEM((kinds, ff, half), BF16),
            pltpu.VMEM((kinds, ff, half), BF16),
            pltpu.VMEM((ff, rows), BF16),
            pltpu.VMEM((ff, rows), BF16),
            pltpu.VMEM((8, rows // 128, 128), jnp.int32),
            pltpu.VMEM((4, 1, rows), jnp.int32),
            pltpu.SemaphoreType.DMA((SEMS,)),
            pltpu.SemaphoreType.DMA((SEMS,)),
            pltpu.SemaphoreType.DMA((16,)),
        ],
        compiler_params=pltpu.CompilerParams(
            collective_id=0, has_side_effects=True, vmem_limit_bytes=67_000_000
        ),
    )(modality.reshape(rows // 128, 128), out_grad, gate_pre.T, up_pre.T, down_weight)
    down_grad = (own.astype(F32) + theirs.astype(F32)) * factor[:, :1, None]
    return down_grad, gate_grad.T, up_grad.T


def solution(mesh):
    torus = Mesh(mesh.devices.reshape(4, 2, 4, 2, 2), AXES)
    fsdp, tensor = ("x", "yl"), ("z", "yh", "c")
    in_specs = (
        P(fsdp),
        P(fsdp, tensor),
        P(fsdp, tensor),
        P(fsdp, tensor),
        P(None, tensor, fsdp),
    )
    out_specs = (P(None, tensor, fsdp), P(fsdp, tensor), P(fsdp, tensor))
    return jax.shard_map(
        shards, mesh=torus, in_specs=in_specs, out_specs=out_specs, check_vma=False
    )
```

time: 178 us -> 131 us (0.74); the launches traced: 176 us -> 131 us
  Pallas kernels: 162 us -> 121 us
  local copies, waits for them, and re-layouts: 13 us -> 3.74 us
  other arithmetic: 0 us -> 5.1 us
    pallas_call x1, Pallas kernels: 162 us -> 121 us  [shards(): pl.pallas_call(kernel, out_shape=(jax.ShapeDtypeStruct((kinds, ff, half),...]
    unnamed x7 -> x6, local copies, waits for them, and re-layouts: 8.9 us -> 2.95 us
    mul x0 -> x1, other arithmetic: none -> 5.1 us  [shards(): down_grad = (own.astype(F32) + theirs.astype(F32)) * factor[:, :1, None]]
    pallas_call x2 -> x0, local copies, waits for them, and re-layouts: 4.14 us -> none  [shards(): pl.pallas_call(kernel, out_shape=(jax.ShapeDtypeStruct((kinds, ff, half),...]
where the time goes in v2:
time: 131 us
  Pallas kernels  121 us (92%)
  other arithmetic  5.1 us (4%)
  local copies, waits for them, and re-layouts  3.74 us (3%)
    pallas_call x1, Pallas kernels, shards(): pl.pallas_call(kernel, out_shape=(jax.ShapeDtypeStruct((kinds, ff, half),...  121 us
    mul x1, other arithmetic, shards(): down_grad = (own.astype(F32) + theirs.astype(F32)) * factor[:, :1, None]  5.1 us
    unnamed x6, local copies, waits for them, and re-layouts  2.95 us

profile of v2, /device:TPU:0, one launch (start us, length us, event | category | flops | bytes accessed | tf_op | source)
XLA Modules:
  0.0 130.7 jit_solution(15840466767210362096)
XLA Ops:
  0.6 121.2 %shard_map.76 = (bf16[3,688,512]{2,1,0:T(8,128)(2,1)}, bf16[3,688,512]{2,1,0:T(8,128)(2,1)}, f32[3,128]{1,0:T(4,128)}, bf16[688,1024]{1,0:T(8,128)(2,1)}, bf16[688,1024]{1,0:T(8,128)(2,1)}) custom-call(s32[8,128]{1,0:T(8,128)} %bitcast.9, bf16[1024,256]{1,0:T(8,128)(2,1)} %og_ref.1, bf16[688,1024]{1,0:T(8,128)(2,1)} %bitcast.5, bf16[688,1024]{1,0:T(8,128)(2,1)} %bitcast.6, ...), custom_call_target="tpu_custom_call" | custom-call | tf_op jit(solution)/shard_map/pallas_call | solution.py:457
  121.9 0.8 slice_reduce_fusion
  122.7 0.0 copy-start.1
  122.7 5.1 %add_multiply_fusion = f32[3,688,512]{2,1,0:T(8,128)} fusion(bf16[3,688,512]{2,1,0:T(8,128)(2,1)} %get-tuple-element.9, bf16[3,688,512]{2,1,0:T(8,128)(2,1)} %get-tuple-element.8, f32[3]{0:T(128)S(1)} %slice_reduce_fusion), kind=kLoop, calls=%fused_computation | loop fusion | flops 4227072 | bytes 8454156 | tf_op jit(solution)/shard_map/mul | solution.py:493
  127.8 0.0 copy-done.1
  127.8 0.0 copy-start
  127.8 1.1 copy.10
  128.9 0.8 copy-done
  129.6 1.1 copy.11
Async XLA Ops:
  122.7 5.1 %copy-start.1 = (bf16[688,1024]{1,0:T(8,128)(2,1)S(1)}, bf16[688,1024]{1,0:T(8,128)(2,1)}, u32[]{:S(2)}) copy-start(bf16[688,1024]{1,0:T(8,128)(2,1)} %get-tuple-element.11) | copy-start | bytes 4227076
  127.8 1.9 %copy-start = (bf16[688,1024]{1,0:T(8,128)(2,1)S(1)}, bf16[688,1024]{1,0:T(8,128)(2,1)}, u32[]{:S(2)}) copy-start(bf16[688,1024]{1,0:T(8,128)(2,1)} %get-tuple-element.12) | copy-start | bytes 4227076

commit v3 on v2

--- a/solution.py
+++ b/solution.py
@@ -10,8 +10,8 @@
 MESH = pl.DeviceIdType.MESH
 F32, BF16 = jnp.float32, jnp.bfloat16
 S1, Z1, YH, UP0, UP1, DN0, DN1, FUP, FDN, CC = 0, 4, 8, 12, 16, 20, 24, 28, 32, 36
-WW, MM, HR, HL, HFR, HFL = 68, 71, 78, 82, 86, 90
-TR, TL, DR1, DL1, DR2, DL2, DW, SEMS = 94, 98, 102, 106, 110, 114, 118, 121
+WW, MM, HR, HL, HFR, HFL = 68, 74, 81, 85, 89, 93
+TR, TL, DR1, DL1, DR2, DL2, DW, SEMS = 97, 101, 105, 109, 113, 117, 121, 124
 
 
 def dot_nt(a, b):
@@ -21,7 +21,7 @@
 def kernel(
     mod_ref, og_ref, gate_ref, up_ref, w_ref, own_ref, theirs_ref, factor_ref, gg_ref, ug_ref,
     zin_ref, s_ref, wv_ref, ht_ref, part_ref, from_left, from_right, hop_left, hop_right,
-    acc_ref, own_v, out_half, gate_v, up_v, mod_all, kind_ref,
+    acc_ref, dw_ref, early_ref, out_half, own_v, gate_v, up_v, mod_all, kind_ref,
     send, recv, local,
 ):
     x, yl, z, yh, c = (lax.axis_index(a) for a in AXES)
@@ -75,21 +75,24 @@
         pltpu.make_async_copy(gate_ref, gate_v, local.at[0]),
         pltpu.make_async_copy(up_ref, up_v, local.at[1]),
     ]
+    group = x * 2 + yl
+    kinds_in = pltpu.make_async_copy(mod_ref, mod_all.at[group], local.at[5])
+    kinds_in.start()
     for copy in loads:
         copy.start()
 
-    def w_copy(m):
-        return rc(w_ref.at[m], wv_ref.at[m, :, tile(yl, half)], WW + m, WW + m, yl=1 - yl)
+    def w_piece(m, i, side):
+        return wv_ref.at[m, (top, low)[i], tile(side, half)]
+
+    def w_copy(m, i):
+        src = w_ref.at[m, (top, low)[i], :]
+        return rc(src, w_piece(m, i, yl), WW + 2 * m + i, WW + 2 * m + i, yl=1 - yl)
 
     def w_local(m):
         return pltpu.make_async_copy(w_ref.at[m], wv_ref.at[m, :, tile(yl, half)], local.at[2 + m])
 
     for m in range(3):
         w_local(m).start()
-    group = x * 2 + yl
-    mod_all[group] = mod_ref[...]
-    for copy in loads:
-        copy.wait()
 
     def make_hidden(k):
         q = order(k)
@@ -97,7 +100,6 @@
         u = up_v[:, tile(q, quarter)].astype(F32)
         ht_ref[q, :, tile(x, quarter)] = (g * jax.nn.sigmoid(g) * u).astype(BF16)
 
-    each(1, make_hidden)
     pl.semaphore_wait(barrier, 12)
 
     def s_first(q, src):
@@ -133,15 +135,13 @@
             along_z(d, False).start()
         home().start()
 
-    w_copy(0).start()
+    w_copy(0, 0).start()
+    w_copy(0, 1).start()
 
     def kinds_copy(i):
         dx, dy = group_steps[i]
         return rc(mod_ref, mod_all.at[group], MM + i, MM + i, x=(x + dx) % 4, yl=(yl + dy) % 2)
 
-    for i in range(7):
-        kinds_copy(i).start()
-
     def h_block(q, src):
         return ht_ref.at[q, :, tile(src, quarter)]
 
@@ -163,9 +163,13 @@
         h_right(k).start()
         h_left(k).start()
 
+    for copy in loads:
+        copy.wait()
+    each(1, make_hidden)
     send_hidden(0)
+    for i in range(7):
+        kinds_copy(i).start()
     each(4, make_hidden, 1)
-    acc_ref[...] = jnp.zeros(acc_ref.shape, F32)
 
     for d in (1, 3, 2):
         @pl.when(passes(d))
@@ -173,7 +177,9 @@
             rc(zin_ref.at[d], zin_ref.at[d], Z1 + d, Z1 + d, z=z).wait_recv()
             along_x(d).start()
 
-    each(4, send_hidden, 1)
+    send_hidden(1)
+    acc_ref[...] = jnp.zeros(acc_ref.shape, F32)
+    dw_ref[...] = jnp.zeros(dw_ref.shape, F32)
 
     def piece(q, e, core, j):
         return s_ref.at[q, tile(source(j), quarter), tile(((yh + e) % 2) * 2 + core, cols)]
@@ -197,8 +203,10 @@
         share(0, 0, j, c).start()
 
     each(4, spread_own)
-    w_copy(1).start()
-    w_copy(2).start()
+    w_copy(1, 0).start()
+    w_copy(1, 1).start()
+    w_copy(2, 0).start()
+    w_copy(2, 1).start()
 
     def pass_hidden(k):
         q = order(k)
@@ -207,7 +215,8 @@
         rc(h_block(q, right), h_block(q, right), HL + k, HL + k, x=left).wait_recv()
         h_on_left(k).start()
 
-    each(1, pass_hidden)
+    pass_hidden(0)
+    send_hidden(2)
 
     def spread_other(j):
         swap(1, j).wait_recv()
@@ -221,8 +230,10 @@
         share(2, 0, j, c).start()
 
     each(4, spread_other)
-    each(3, pass_hidden, 1)
-
+    pass_hidden(1)
+    send_hidden(3)
+
+    kinds_in.wait()
     for i in range(7):
         dx, dy = group_steps[i]
         src = ((x + 4 - dx) % 4) * 2 + (yl + dy) % 2
@@ -263,7 +274,11 @@
         hidden_in(k)
 
         def one(m):
-            acc_ref[m] += jnp.dot(marked(q, m), s_ref[q], preferred_element_type=F32)
+            rows_marked = marked(q, m)
+            for ref, side in ((acc_ref, 1 - yl), (dw_ref, yl)):
+                ref[m] += jnp.dot(
+                    rows_marked, s_ref[q, :, tile(side, half)], preferred_element_type=F32
+                )
 
         each(3, one)
 
@@ -282,15 +297,39 @@
         ring(far, 1, j, FDN, down_z).wait_recv()
         share(3, 1, j, c).start()
 
+    def two_blocks(p):
+        return (x + 2 + p) % 4, (x + 1 + 3 * p) % 4
+
+    def d_hidden_part(q, p, at):
+        one, two = two_blocks(p)
+        block = jnp.concatenate(
+            [s_ref[q, tile(one, quarter), at], s_ref[q, tile(two, quarter), at]], axis=0
+        )
+        kind = jnp.concatenate(
+            [kind_ref[q, :, tile(one, quarter)], kind_ref[q, :, tile(two, quarter)]], axis=1
+        )
+        got = dot_nt(wv_ref[0, :, at], block)
+        for m in range(1, 3):
+            got = jnp.where(kind == m, dot_nt(wv_ref[m, :, at], block), got)
+        return got
+
+    def early(p):
+        early_ref[p] = d_hidden_part(z, p, tile(yl, half))
+
+    add_quarter(0)
     each(4, spread_near)
-    each(4, pass_hidden, 3)
-    each(2, add_quarter)
-    each(4, spread_far)
-    each(3, add_quarter, 2)
     for m in range(3):
         w_local(m).wait()
-        theirs = wv_ref.at[m, :, tile(1 - yl, half)]
-        rc(theirs, theirs, WW + m, WW + m, yl=1 - yl).wait_recv()
+    each(2, early)
+    pass_hidden(2)
+    add_quarter(1)
+    each(4, spread_far)
+    pass_hidden(3)
+    add_quarter(2)
+    for m in range(3):
+        for i in range(2):
+            theirs = w_piece(m, i, 1 - yl)
+            rc(theirs, theirs, WW + 2 * m + i, WW + 2 * m + i, yl=1 - yl).wait_recv()
 
     def hop(k, to_right):
         q = order(k)
@@ -322,65 +361,82 @@
         ).astype(BF16)
         gives(k, 3).start()
 
-    def d_hidden(k):
-        q = order(k)
-
-        def pair(p):
-            block = s_ref[q, tile(p, half), :]
-            kind = kind_ref[q, :, tile(p, half)]
-            got = dot_nt(wv_ref[0], block)
-            for m in range(1, 3):
-                got = jnp.where(kind == m, dot_nt(wv_ref[m], block), got)
-            got = got.astype(BF16)
-            part_ref[2 * p, q] = got[:, :quarter]
-            part_ref[2 * p + 1, q] = got[:, quarter:]
-
-        each(2, pair)
+    def keep(q, p, got):
+        got = got.astype(BF16)
+        one, two = two_blocks(p)
+        part_ref[one, q] = got[:, :quarter]
+        part_ref[two, q] = got[:, quarter:]
+
+    def send_first(k):
         hop(k, True).start()
         hop(k, False).start()
         gives(k, 0).start()
+
+    def first_pair(p):
+        keep(z, p, early_ref[p] + d_hidden_part(z, p, tile(1 - yl, half)))
+
+        @pl.when(p == 0)
+        def _():
+            send_first(0)
+
+    def d_hidden(k):
+        q = order(k)
+
+        def pair(p):
+            keep(q, p, d_hidden_part(q, p, slice(None)))
+
+            @pl.when(p == 0)
+            def _():
+                send_first(k)
+                relay(k - 1)
+
+        each(2, pair)
         gives(k, 1).start()
 
     def dw_copy(m):
         return rc(out_half.at[m], theirs_ref.at[m], DW + m, DW + m, yl=1 - yl)
 
+    def last_sum(ref, m, side):
+        q = order(3)
+        return ref[m] + jnp.dot(
+            marked(q, m), s_ref[q, :, tile(side, half)], preferred_element_type=F32
+        )
+
     def own_out(m):
-        return pltpu.make_async_copy(own_v.at[m], own_ref.at[m], local.at[5 + m])
-
-    def last_sum(m, side):
-        q = order(3)
-        at = tile(side, half)
-        return acc_ref[m, :, at] + jnp.dot(
-            marked(q, m), s_ref[q, :, at], preferred_element_type=F32
-        )
-
-    def other_half(m):
-        out_half[m] = last_sum(m, 1 - yl).astype(BF16)
-        dw_copy(m).start()
-
-    def own_half(m):
-        own_v[m] = last_sum(m, yl).astype(BF16)
-        own_out(m).start()
-
-    d_hidden(0)
-    block_in(3)
-    hidden_in(3)
-    each(3, other_half)
-
-    def more_d_hidden(k):
-        d_hidden(k)
-        relay(k - 1)
-
-    each(4, more_d_hidden, 1)
-    each(3, own_half)
-    relay(3)
+        return pltpu.make_async_copy(own_v.at[m], own_ref.at[m], local.at[6 + m])
 
     def grads_out(k):
         at = tile(order(k), quarter)
         return (
-            pltpu.make_async_copy(up_v.at[:, at], ug_ref.at[:, at], local.at[8 + k]),
-            pltpu.make_async_copy(gate_v.at[:, at], gg_ref.at[:, at], local.at[12 + k]),
-        )
+            pltpu.make_async_copy(up_v.at[:, at], ug_ref.at[:, at], local.at[9 + k]),
+            pltpu.make_async_copy(gate_v.at[:, at], gg_ref.at[:, at], local.at[13 + k]),
+        )
+
+    def other_half(m):
+        out_half[m] = last_sum(acc_ref, m, 1 - yl).astype(BF16)
+        dw_copy(m).start()
+
+    def own_half(m):
+        own_v[m] = last_sum(dw_ref, m, yl).astype(BF16)
+        own_out(m).start()
+
+    block_in(3)
+    hidden_in(3)
+    other_half(0)
+    each(2, first_pair)
+    gives(0, 1).start()
+
+    def steady(k):
+        @pl.when(k < 3)
+        def _():
+            other_half(k)
+
+        d_hidden(k)
+
+    each(4, steady, 1)
+    each(1, own_half)
+    relay(3)
+    each(3, own_half, 1)
 
     def finish(k):
         q = order(k)
@@ -443,8 +499,48 @@
 
     each(4, drain)
     for m in range(3):
-        w_copy(m).wait_send()
+        w_copy(m, 0).wait_send()
+        w_copy(m, 1).wait_send()
         dw_copy(m).wait_send()
+
+
+def store(
+    own_ref, theirs_ref, factor_ref, gg_ref, ug_ref, dw_out, gg_out, ug_out,
+    own_v, theirs_v, dw_v, gg_v, ug_v, come, go,
+):
+    ff = gg_ref.shape[0]
+    cut = (ff // 2 + 15) // 16 * 16
+    parts = [(m, at) for m in range(3) for at in (pl.ds(0, cut), pl.ds(cut, ff - cut))]
+    copy = pltpu.make_async_copy
+    grads_in = [copy(gg_ref, gg_v, come.at[0]), copy(ug_ref, ug_v, come.at[1])]
+    grads_go = [copy(gg_v, gg_out, go.at[0]), copy(ug_v, ug_out, go.at[1])]
+    sums_in = [
+        (
+            copy(own_ref.at[m, at, :], own_v.at[m, at, :], come.at[2 + 2 * i]),
+            copy(theirs_ref.at[m, at, :], theirs_v.at[m, at, :], come.at[3 + 2 * i]),
+        )
+        for i, (m, at) in enumerate(parts)
+    ]
+    sums_go = [
+        copy(dw_v.at[m, at, :], dw_out.at[m, at, :], go.at[2 + i]) for i, (m, at) in enumerate(parts)
+    ]
+    for one in grads_in:
+        one.start()
+    for pair in sums_in:
+        for one in pair:
+            one.start()
+    for i in range(2):
+        grads_in[i].wait()
+        grads_go[i].start()
+    for i, (m, at) in enumerate(parts):
+        for one in sums_in[i]:
+            one.wait()
+        dw_v[m, at, :] = (own_v[m, at, :].astype(F32) + theirs_v[m, at, :].astype(F32)) * (
+            factor_ref[m : m + 1, :1]
+        )
+        sums_go[i].start()
+    for one in grads_go + sums_go:
+        one.wait()
 
 
 def shards(modality, out_grad, gate_pre, up_pre, down_weight):
@@ -452,19 +548,20 @@
     kinds, ff, half = down_weight.shape
     quarter = rows // 4
     cut = (ff // 2 + 15) // 16 * 16
-    anywhere = pl.BlockSpec(memory_space=pl.ANY)
+    hbm = pl.BlockSpec(memory_space=pltpu.HBM)
     vmem = pl.BlockSpec(memory_space=pltpu.VMEM)
-    own, theirs, factor, gate_grad, up_grad = pl.pallas_call(
+    grad_shapes = (jax.ShapeDtypeStruct((ff, rows), BF16),) * 2
+    shapes = (
+        jax.ShapeDtypeStruct((kinds, ff, half), BF16),
+        jax.ShapeDtypeStruct((kinds, ff, half), BF16),
+        jax.ShapeDtypeStruct((kinds, 128), F32),
+        *grad_shapes,
+    )
+    results = pl.pallas_call(
         kernel,
-        out_shape=(
-            jax.ShapeDtypeStruct((kinds, ff, half), BF16),
-            jax.ShapeDtypeStruct((kinds, ff, half), BF16),
-            jax.ShapeDtypeStruct((kinds, 128), F32),
-            jax.ShapeDtypeStruct((ff, rows), BF16),
-            jax.ShapeDtypeStruct((ff, rows), BF16),
-        ),
-        in_specs=[vmem, anywhere, anywhere, anywhere, anywhere],
-        out_specs=(anywhere, anywhere, vmem, anywhere, anywhere),
+        out_shape=shapes,
+        in_specs=[hbm] * 5,
+        out_specs=(hbm, hbm, vmem, hbm, hbm),
         scratch_shapes=[
             pltpu.VMEM((4, quarter, cols), BF16),
             pltpu.VMEM((4, rows, 4 * cols), BF16),
@@ -475,7 +572,9 @@
             pltpu.VMEM((4, ff, quarter), BF16),
             pltpu.VMEM((4, cut, quarter), BF16),
             pltpu.VMEM((4, ff - cut, quarter), BF16),
-            pltpu.VMEM((kinds, ff, 2 * half), F32),
+            pltpu.VMEM((kinds, ff, half), F32),
+            pltpu.VMEM((kinds, ff, half), F32),
+            pltpu.VMEM((2, ff, half), F32),
             pltpu.VMEM((kinds, ff, half), BF16),
             pltpu.VMEM((kinds, ff, half), BF16),
             pltpu.VMEM((ff, rows), BF16),
@@ -484,13 +583,28 @@
             pltpu.VMEM((4, 1, rows), jnp.int32),
             pltpu.SemaphoreType.DMA((SEMS,)),
             pltpu.SemaphoreType.DMA((SEMS,)),
-            pltpu.SemaphoreType.DMA((16,)),
+            pltpu.SemaphoreType.DMA((17,)),
         ],
         compiler_params=pltpu.CompilerParams(
-            collective_id=0, has_side_effects=True, vmem_limit_bytes=67_000_000
+            collective_id=0, has_side_effects=True, vmem_limit_bytes=60_000_000
         ),
     )(modality.reshape(rows // 128, 128), out_grad, gate_pre.T, up_pre.T, down_weight)
-    down_grad = (own.astype(F32) + theirs.astype(F32)) * factor[:, :1, None]
+    down_grad, gate_grad, up_grad = pl.pallas_call(
+        store,
+        out_shape=(jax.ShapeDtypeStruct((kinds, ff, half), F32), *grad_shapes),
+        in_specs=[hbm, hbm, vmem, hbm, hbm],
+        out_specs=(hbm, hbm, hbm),
+        scratch_shapes=[
+            pltpu.VMEM((kinds, ff, half), BF16),
+            pltpu.VMEM((kinds, ff, half), BF16),
+            pltpu.VMEM((kinds, ff, half), F32),
+            pltpu.VMEM((ff, rows), BF16),
+            pltpu.VMEM((ff, rows), BF16),
+            pltpu.SemaphoreType.DMA((14,)),
+            pltpu.SemaphoreType.DMA((8,)),
+        ],
+        compiler_params=pltpu.CompilerParams(vmem_limit_bytes=60_000_000),
+    )(*results)
     return down_grad, gate_grad.T, up_grad.T
 
 

time: 131 us -> 126 us (0.962)
  other arithmetic: 5.1 us -> 0 us
  Pallas kernels: 121 us -> 125 us
  local copies, waits for them, and re-layouts: 3.74 us -> 0 us
    mul x1 -> x0, other arithmetic: 5.1 us -> none  [shards(): down_grad = (own.astype(F32) + theirs.astype(F32)) * factor[:, :1, None]]
    pallas_call x1 -> x2, Pallas kernels: 121 us -> 125 us  [the longest x1 118 us: shards(): pl.pallas_call(kernel, out_shape=shapes, in_specs=[hbm] * 5, out_specs=(h...]
    unnamed x6 -> x0, local copies, waits for them, and re-layouts: 2.95 us -> none
where the time goes in v3:
time: 126 us
  Pallas kernels  125 us (99%)
    pallas_call x1, Pallas kernels, shards(): pl.pallas_call(kernel, out_shape=shapes, in_specs=[hbm] * 5, out_specs=(h...  118 us
    pallas_call x1, Pallas kernels, shards(): pl.pallas_call(store, out_shape=(jax.ShapeDtypeStruct((kinds, ff, half),...  6.69 us

profile of v3, /device:TPU:0, one launch (start us, length us, event | category | flops | bytes accessed | tf_op | source)
XLA Modules:
  0.0 125.5 jit_solution(3228576692585648174)
XLA Ops:
  0.6 118.2 %shard_map.76 = (bf16[3,688,512]{2,1,0:T(8,128)(2,1)}, bf16[3,688,512]{2,1,0:T(8,128)(2,1)}, f32[3,128]{1,0:T(4,128)}, bf16[688,1024]{1,0:T(8,128)(2,1)}, bf16[688,1024]{1,0:T(8,128)(2,1)}) custom-call(s32[8,128]{1,0:T(8,128)} %bitcast.7, bf16[1024,256]{1,0:T(8,128)(2,1)} %og_ref.1, bf16[688,1024]{1,0:T(8,128)(2,1)} %bitcast.5, bf16[688,1024]{1,0:T(8,128)(2,1)} %bitcast.6, ...), custom_call_target="tpu_custom_call" | custom-call | tf_op jit(solution)/shard_map/pallas_call | solution.py:560
  118.9 6.7 %shard_map.77 = (f32[3,688,512]{2,1,0:T(8,128)}, bf16[688,1024]{1,0:T(8,128)(2,1)}, bf16[688,1024]{1,0:T(8,128)(2,1)}) custom-call(bf16[3,688,512]{2,1,0:T(8,128)(2,1)} %get-tuple-element.11.own_ref, bf16[3,688,512]{2,1,0:T(8,128)(2,1)} %get-tuple-element.12.theirs_ref, f32[3,128]{1,0:T(4,128)} %get-tuple-element.13.factor_ref, ...), custom_call_target="tpu_custom_call" | custom-call | tf_op jit(solution)/shard_map/pallas_call | solution.py:592

commit v4 on v3

--- a/solution.py
+++ b/solution.py
@@ -10,8 +10,8 @@
 MESH = pl.DeviceIdType.MESH
 F32, BF16 = jnp.float32, jnp.bfloat16
 S1, Z1, YH, UP0, UP1, DN0, DN1, FUP, FDN, CC = 0, 4, 8, 12, 16, 20, 24, 28, 32, 36
-WW, MM, HR, HL, HFR, HFL = 68, 74, 81, 85, 89, 93
-TR, TL, DR1, DL1, DR2, DL2, DW, SEMS = 97, 101, 105, 109, 113, 117, 121, 124
+WW, MM, HR, HL, HFR, HFL = 68, 80, 87, 91, 95, 99
+TR, TL, DR1, DL1, DR2, DL2, DW, SEMS = 103, 107, 111, 115, 119, 123, 127, 130
 
 
 def dot_nt(a, b):
@@ -81,12 +81,23 @@
     for copy in loads:
         copy.start()
 
-    def w_piece(m, i, side):
-        return wv_ref.at[m, (top, low)[i], tile(side, half)]
-
-    def w_copy(m, i):
-        src = w_ref.at[m, (top, low)[i], :]
-        return rc(src, w_piece(m, i, yl), WW + 2 * m + i, WW + 2 * m + i, yl=1 - yl)
+    fourth = (ff // 4 + 15) // 16 * 16
+    w_parts = [
+        (m, pl.ds(i * fourth, fourth if i < 3 else ff - 3 * fourth))
+        for m in range(3) for i in range(4)
+    ]
+
+    def w_piece(i, side):
+        m, at = w_parts[i]
+        return wv_ref.at[m, at, tile(side, half)]
+
+    def w_copy(i):
+        m, at = w_parts[i]
+        return rc(w_ref.at[m, at, :], w_piece(i, yl), WW + i, WW + i, yl=1 - yl)
+
+    def send_weights(first, last):
+        for i in range(first, last):
+            w_copy(i).start()
 
     def w_local(m):
         return pltpu.make_async_copy(w_ref.at[m], wv_ref.at[m, :, tile(yl, half)], local.at[2 + m])
@@ -135,8 +146,7 @@
             along_z(d, False).start()
         home().start()
 
-    w_copy(0, 0).start()
-    w_copy(0, 1).start()
+    send_weights(0, 4)
 
     def kinds_copy(i):
         dx, dy = group_steps[i]
@@ -169,17 +179,15 @@
     send_hidden(0)
     for i in range(7):
         kinds_copy(i).start()
-    each(4, make_hidden, 1)
-
     for d in (1, 3, 2):
         @pl.when(passes(d))
         def _():
             rc(zin_ref.at[d], zin_ref.at[d], Z1 + d, Z1 + d, z=z).wait_recv()
             along_x(d).start()
 
+    make_hidden(1)
+
     send_hidden(1)
-    acc_ref[...] = jnp.zeros(acc_ref.shape, F32)
-    dw_ref[...] = jnp.zeros(dw_ref.shape, F32)
 
     def piece(q, e, core, j):
         return s_ref.at[q, tile(source(j), quarter), tile(((yh + e) % 2) * 2 + core, cols)]
@@ -193,6 +201,15 @@
     def share(k, e, j, core):
         i = CC + 8 * k + 4 * e + j
         return rc(piece(order(k), e, core, j), piece(order(k), e, core, j), i, i, c=1 - c)
+
+    def passed(q, e, j, to_up):
+        return ring(q, e, j, FUP + 2 * e, up_z) if to_up else ring(q, e, j, FDN + 2 * e - 2, down_z)
+
+    def pass_on(e, j):
+        if j < 2:
+            passed(down_z, e, j, True).start()
+        else:
+            passed(up_z, e, j, False).start()
 
     def spread_own(j):
         dst = s_first(z, source(j))
@@ -202,11 +219,10 @@
         ring(z, 0, j, DN0, down_z).start()
         share(0, 0, j, c).start()
 
-    each(4, spread_own)
-    w_copy(1, 0).start()
-    w_copy(1, 1).start()
-    w_copy(2, 0).start()
-    w_copy(2, 1).start()
+    spread_own(0)
+    send_weights(4, 4)
+    each(4, spread_own, 1)
+    send_weights(4, 12)
 
     def pass_hidden(k):
         q = order(k)
@@ -215,6 +231,7 @@
         rc(h_block(q, right), h_block(q, right), HL + k, HL + k, x=left).wait_recv()
         h_on_left(k).start()
 
+    each(4, make_hidden, 2)
     pass_hidden(0)
     send_hidden(2)
 
@@ -224,12 +241,13 @@
         ring(z, 1, j, DN1, down_z).start()
         share(0, 1, j, c).start()
         ring(down_z, 0, j, UP0, up_z).wait_recv()
-        ring(down_z, 0, j, FUP, up_z).start()
         share(1, 0, j, c).start()
         ring(up_z, 0, j, DN0, down_z).wait_recv()
         share(2, 0, j, c).start()
-
-    each(4, spread_other)
+        pass_on(0, j)
+
+    for j in range(4):
+        spread_other(j)
     pass_hidden(1)
     send_hidden(3)
 
@@ -268,7 +286,7 @@
     def marked(q, m):
         return ht_ref[q] * (kind_ref[q] == m).astype(F32).astype(BF16)
 
-    def add_quarter(k):
+    def add_quarter(k, opening=False):
         q = order(k)
         block_in(k)
         hidden_in(k)
@@ -276,26 +294,26 @@
         def one(m):
             rows_marked = marked(q, m)
             for ref, side in ((acc_ref, 1 - yl), (dw_ref, yl)):
-                ref[m] += jnp.dot(
+                part = jnp.dot(
                     rows_marked, s_ref[q, :, tile(side, half)], preferred_element_type=F32
                 )
+                ref[m] = part if opening else ref[m] + part
 
         each(3, one)
 
     def spread_near(j):
         ring(up_z, 1, j, DN1, down_z).wait_recv()
-        ring(up_z, 1, j, FDN, down_z).start()
         share(2, 1, j, c).start()
         ring(down_z, 1, j, UP1, up_z).wait_recv()
         share(1, 1, j, c).start()
+        pass_on(1, j)
 
     far = (z + 2) % 4
 
     def spread_far(j):
-        ring(far, 0, j, FUP, up_z).wait_recv()
-        share(3, 0, j, c).start()
-        ring(far, 1, j, FDN, down_z).wait_recv()
-        share(3, 1, j, c).start()
+        for e in range(2):
+            passed(far, e, j, j < 2).wait_recv()
+            share(3, e, j, c).start()
 
     def two_blocks(p):
         return (x + 2 + p) % 4, (x + 1 + 3 * p) % 4
@@ -316,20 +334,21 @@
     def early(p):
         early_ref[p] = d_hidden_part(z, p, tile(yl, half))
 
-    add_quarter(0)
-    each(4, spread_near)
+    add_quarter(0, True)
+    for j in range(4):
+        spread_near(j)
     for m in range(3):
         w_local(m).wait()
     each(2, early)
     pass_hidden(2)
     add_quarter(1)
-    each(4, spread_far)
+    for j in range(4):
+        spread_far(j)
     pass_hidden(3)
     add_quarter(2)
-    for m in range(3):
-        for i in range(2):
-            theirs = w_piece(m, i, 1 - yl)
-            rc(theirs, theirs, WW + 2 * m + i, WW + 2 * m + i, yl=1 - yl).wait_recv()
+    for i in range(12):
+        theirs = w_piece(i, 1 - yl)
+        rc(theirs, theirs, WW + i, WW + i, yl=1 - yl).wait_recv()
 
     def hop(k, to_right):
         q = order(k)
@@ -485,7 +504,7 @@
         swap(0, k).wait_send()
         for q, e, base, to in (
             (z, 0, UP0, up_z), (z, 1, UP1, up_z), (z, 0, DN0, down_z),
-            (z, 1, DN1, down_z), (down_z, 0, FUP, up_z), (up_z, 1, FDN, down_z),
+            (z, 1, DN1, down_z),
         ):
             ring(q, e, k, base, to).wait_send()
         for copy in (h_right(k), h_left(k), h_on_right(k), h_on_left(k)):
@@ -497,10 +516,13 @@
         for i in range(4):
             gives(k, i).wait_send()
 
+    for e in range(2):
+        for j in range(4):
+            passed((down_z, up_z)[j // 2], e, j, j < 2).wait_send()
     each(4, drain)
+    for i in range(12):
+        w_copy(i).wait_send()
     for m in range(3):
-        w_copy(m, 0).wait_send()
-        w_copy(m, 1).wait_send()
         dw_copy(m).wait_send()
 
 

time: 126 us -> 126 us (level)
  no operation moved by 1% of the time
where the time goes in v4:
time: 126 us
  Pallas kernels  125 us (99%)
    pallas_call x1, Pallas kernels, shards(): pl.pallas_call(kernel, out_shape=shapes, in_specs=[hbm] * 5, out_specs=(h...  118 us
    pallas_call x1, Pallas kernels, shards(): pl.pallas_call(store, out_shape=(jax.ShapeDtypeStruct((kinds, ff, half),...  6.69 us

profile of v4, /device:TPU:0, one launch (start us, length us, event | category | flops | bytes accessed | tf_op | source)
XLA Modules:
  0.0 125.7 jit_solution(589738751820556979)
XLA Ops:
  0.6 118.3 %shard_map.76 = (bf16[3,688,512]{2,1,0:T(8,128)(2,1)}, bf16[3,688,512]{2,1,0:T(8,128)(2,1)}, f32[3,128]{1,0:T(4,128)}, bf16[688,1024]{1,0:T(8,128)(2,1)}, bf16[688,1024]{1,0:T(8,128)(2,1)}) custom-call(s32[8,128]{1,0:T(8,128)} %bitcast.7, bf16[1024,256]{1,0:T(8,128)(2,1)} %og_ref.1, bf16[688,1024]{1,0:T(8,128)(2,1)} %bitcast.5, bf16[688,1024]{1,0:T(8,128)(2,1)} %bitcast.6, ...), custom_call_target="tpu_custom_call" | custom-call | tf_op jit(solution)/shard_map/pallas_call | solution.py:582
  119.0 6.7 %shard_map.77 = (f32[3,688,512]{2,1,0:T(8,128)}, bf16[688,1024]{1,0:T(8,128)(2,1)}, bf16[688,1024]{1,0:T(8,128)(2,1)}) custom-call(bf16[3,688,512]{2,1,0:T(8,128)(2,1)} %get-tuple-element.11.own_ref, bf16[3,688,512]{2,1,0:T(8,128)(2,1)} %get-tuple-element.12.theirs_ref, f32[3,128]{1,0:T(4,128)} %get-tuple-element.13.factor_ref, ...), custom_call_target="tpu_custom_call" | custom-call | tf_op jit(solution)/shard_map/pallas_call | solution.py:614
